TPU v7x, 256 devices: a whole 4x4x8 slice. The times are simulated.
256 devices in a mesh: grp: 32 (over z, x_lo, core), tile: 8 (over x_hi, y).
Axes of the slice: x: 4 (x_hi: 2, x_lo: 2; x = x_hi * 2 + x_lo), y: 4, z: 8, core: 2. Of those that a mesh axis runs over, the one named last changes fastest.
Arguments:
- spectrum: float32 [1152, 256, 512], P(None, 'tile', 'grp'), may hold values from 0.05 to 2
- matrices: bfloat16 [8, 32, 2, 1152, 1152], P('tile', 'grp'), may hold values from -0.1875 to 0.1875
- ownership: int32 [256, 512], P('tile', 'grp'), may hold values from 0 to 1
- land_mask: int32 [256, 512], P('tile', 'grp'), may hold values 0 or 1
- courant: float32 [2, 1152], replicated, may hold values from -0.45 to 0.45
- stokes_weight: bfloat16 [1152, 256], replicated, may hold values from -0.1875 to 0.1875
- ocean: float32 [4, 256, 512, 128], P(None, 'tile', 'grp'), may hold values from -6 to 6
Outputs:
- spectrum_out: float32 [1152, 256, 512], P(None, 'tile', 'grp')
- ocean_out: float32 [4, 256, 512, 128], P(None, 'tile', 'grp')
All inputs are finite; a program needn't handle non-finite values. No bound on the sum of `land_mask` on one device may be relied on, other than what follows from the above.
Results may differ from a plain program's by a relative error of at most 0.0021.
Values sent between devices are 32-bit elements; how exact they have to be, the bound alone decides.
A program may use at most 128 MiB of HBM per device.

v0:
```python
import jax
import jax.numpy as jnp
from jax import lax
from jax.sharding import PartitionSpec as P

STEPS = 2


current_gain = 0.2
source_gain = 0.5
mixing_side = 0.15
mixing_depth = 0.2
rotation = 0.3
transport = 0.5


def with_halo(cells, sides, width):
    for axis, dim in sides:
        count = lax.axis_size(axis)
        ends = count - 1
        head = lax.slice_in_dim(cells, 0, width, axis=dim)
        tail = lax.slice_in_dim(cells, cells.shape[dim] - width, cells.shape[dim], axis=dim)
        cells = jnp.concatenate(
            [
                lax.ppermute(tail, axis, [(i, (i + 1) % count) for i in range(ends)]),
                cells,
                lax.ppermute(head, axis, [((i + 1) % count, i) for i in range(ends)]),
            ],
            axis=dim,
        )
    return cells


def upwind(padded, speed_x, speed_y, sea_mask):
    middle = padded[:, 1:-1, 1:-1]
    western = padded[:, 1:-1, :-2]
    eastern = padded[:, 1:-1, 2:]
    northern = padded[:, :-2, 1:-1]
    southern = padded[:, 2:, 1:-1]
    flux = jnp.maximum(speed_x, 0.0) * (middle - western) + jnp.minimum(speed_x, 0.0) * (
        eastern - middle
    )
    flux = (
        flux
        + jnp.maximum(speed_y, 0.0) * (middle - northern)
        + jnp.minimum(speed_y, 0.0) * (southern - middle)
    )
    return sea_mask[None] * (middle - flux)


def ocean_step(fields, padded, drift, sea_mask):
    northern = padded[:, :-2, 1:-1]
    southern = padded[:, 2:, 1:-1]
    western = padded[:, 1:-1, :-2]
    eastern = padded[:, 1:-1, 2:]
    lateral = northern + southern + western + eastern - 4.0 * fields
    column = jnp.pad(fields, ((0, 0), (0, 0), (0, 0), (1, 1)))
    vertical = column[..., 2:] + column[..., :-2] - 2.0 * fields
    mixing = mixing_side * lateral + mixing_depth * vertical
    tend_u = mixing[0] + rotation * (fields[1] + drift[1])
    tend_v = mixing[1] - rotation * (fields[0] + drift[0])
    grad_x = 0.5 * (eastern[2:] - western[2:])
    grad_y = 0.5 * (southern[2:] - northern[2:])
    tend_tracer = mixing[2:] - transport * (drift[0][None] * grad_x + drift[1][None] * grad_y)
    tendency = jnp.concatenate([tend_u[None], tend_v[None], tend_tracer], 0)
    return fields + sea_mask[None, :, :, None] * tendency


def local(spectrum, matrices, ownership, land_mask, courant, stokes_weight, ocean):
    sea_mask = land_mask.astype(jnp.float32)
    matrix_set = matrices.reshape(matrices.shape[2:])
    count = matrix_set.shape[0]
    bins_all = spectrum.shape[0]
    block_rows = spectrum.shape[1]
    block_cols = spectrum.shape[2]
    levels_count = ocean.shape[3]
    owner_flat = ownership.reshape(1, 1, block_rows * block_cols)
    choices_range = jnp.arange(count, dtype=jnp.int32)[:, None, None]
    profile = stokes_weight.reshape(bins_all, 2, levels_count)
    energy = spectrum
    fields = ocean
    for step in range(STEPS):
        current = fields[0:2, :, :, 0]
        speed_x = courant[0][:, None, None] + current_gain * current[0][None]
        speed_y = courant[1][:, None, None] + current_gain * current[1][None]
        padded = with_halo(energy, (("grp", 2), ("tile", 1)), 1)
        advected = upwind(padded, speed_x, speed_y, sea_mask)
        flattened = advected.astype(jnp.bfloat16).reshape(bins_all, block_rows * block_cols)
        products = jnp.einsum(
            "mab,bp->map", matrix_set, flattened, preferred_element_type=jnp.float32
        )
        select = (owner_flat == choices_range).astype(jnp.float32)
        source = jnp.sum(select * products, axis=0).reshape(bins_all, block_rows, block_cols)
        energy = sea_mask[None] * (advected + source_gain * source)
        drift = jnp.einsum(
            "brc,bkl->krcl",
            energy.astype(jnp.bfloat16),
            profile,
            preferred_element_type=jnp.float32,
        )
        padded_ocean = with_halo(fields, (("grp", 2), ("tile", 1)), 1)
        fields = ocean_step(fields, padded_ocean, drift, sea_mask)
    return (energy, fields)


def solution(mesh):
    in_specs = (
        P(None, "tile", "grp"),
        P("tile", "grp", None, None, None),
        P("tile", "grp"),
        P("tile", "grp"),
        P(),
        P(),
        P(None, "tile", "grp", None),
    )
    out_specs = (P(None, "tile", "grp"), P(None, "tile", "grp", None))
    return jax.shard_map(local, mesh=mesh, in_specs=in_specs, out_specs=out_specs, check_vma=False)
```

profile of v0, /device:TPU:132, one launch (start us, length us, event | category | flops | bytes accessed | tf_op | source)
XLA Modules:
  0.0 110.0 jit_solution(6125336069913867928)
XLA Ops:
  0.6 1.9 %fusion.92 = (f32[1152,32,1]{0,2,1:T(1,128)S(1)}, f32[1152,32,1]{0,2,1:T(1,128)S(1)}) fusion(f32[1152,32,16]{0,2,1:T(8,128)} %param.7), kind=kLoop, calls=%fused_computation.173 | loop fusion | bytes 589824 | tf_op jit(solution)/shard_map/slice | solution.py:22
  2.6 2.2 %collective-permute-start.1 = (f32[1152,32,1]{0,1,2:T(8,128)S(1)}, f32[1152,32,1]{0,1,2:T(8,128)S(1)}, u32[]{:S(2)}, u32[]{:S(2)}) collective-permute-start(f32[1152,32,1]{0,1,2:T(8,128)S(1)} %copy.138), channel_id=1, source_target_pairs={{8,0},{16,8},{24,16},{32,24},{40,32},{48,40},{56,48},{64,56},{72,6... | collective-permute-start | bytes 442376 | tf_op jit(solution)/shard_map/ppermute | solution.py:27
  4.8 0.7 copy.137
  5.5 2.2 %collective-permute-start = (f32[1152,32,1]{0,1,2:T(8,128)}, f32[1152,32,1]{0,1,2:T(8,128)}, u32[]{:S(2)}, u32[]{:S(2)}) collective-permute-start(f32[1152,32,1]{0,1,2:T(8,128)} %copy.137), channel_id=1, source_target_pairs={{0,8},{8,16},{16,24},{24,32},{32,40},{40,48},{48,56},{56,64},{64,7... | collective-permute-start | bytes 442376 | tf_op jit(solution)/shard_map/ppermute | solution.py:25
  7.7 1.6 %copy.90 = f32[4,32,16,128]{3,1,0,2:T(8,128)S(1)} copy(f32[4,32,16,128]{3,2,1,0:T(8,128)} %param.13) | data formatting | bytes 2097152 | tf_op args[6]
  9.3 0.6 fusion.95
  10.0 3.0 %collective-permute-start.4 = (f32[4,32,1,128]{3,1,0,2:T(8,128)}, f32[4,32,1,128]{3,1,0,2:T(8,128)}, u32[]{:S(2)}, u32[]{:S(2)}) collective-permute-start(f32[4,32,1,128]{3,1,0,2:T(8,128)} %get-tuple-element.42), channel_id=1, source_target_pairs={{0,8},{8,16},{16,24},{24,32},{32,40},{40,48},{48,56},{56,64},{64,7... | collective-permute-start | bytes 196616 | tf_op jit(solution)/shard_map/ppermute | solution.py:25
  12.9 4.7 %collective-permute-start.5 = (f32[4,32,1,128]{3,1,0,2:T(8,128)}, f32[4,32,1,128]{3,1,0,2:T(8,128)}, u32[]{:S(2)}, u32[]{:S(2)}) collective-permute-start(f32[4,32,1,128]{3,1,0,2:T(8,128)} %get-tuple-element.41), channel_id=1, source_target_pairs={{8,0},{16,8},{24,16},{32,24},{40,32},{48,40},{56,48},{64,56},{72,6... | collective-permute-start | bytes 196616 | tf_op jit(solution)/shard_map/ppermute | solution.py:27
  17.7 0.3 copy.130
  18.6 0.8 constant_dynamic-update-slice_fusion.4
  19.4 0.5 constant_dynamic-update-slice_fusion.6
  19.9 1.1 constant_dynamic-update-slice_fusion.5
  21.1 3.5 %collective-permute-start.6 = (f32[4,1,18,128]{3,1,0,2:T(1,128)S(1)}, f32[4,1,18,128]{3,1,0,2:T(1,128)S(1)}, u32[]{:S(2)}, u32[]{:S(2)}) collective-permute-start(f32[4,1,18,128]{3,1,0,2:T(1,128)S(1)} %get-tuple-element.33), channel_id=1, source_target_pairs={{0,1},{1,2},{2,3},{3,4},{4,5},{5,6},{6,7},{8,9},{9,10},{10,11},{11... | collective-permute-start | bytes 110600 | tf_op jit(solution)/shard_map/ppermute | solution.py:25
  24.6 6.0 %collective-permute-start.7 = (f32[4,1,18,128]{3,1,0,2:T(1,128)S(1)}, f32[4,1,18,128]{3,1,0,2:T(1,128)S(1)}, u32[]{:S(2)}, u32[]{:S(2)}) collective-permute-start(f32[4,1,18,128]{3,1,0,2:T(1,128)S(1)} %get-tuple-element.32), channel_id=1, source_target_pairs={{1,0},{2,1},{3,2},{4,3},{5,4},{6,5},{7,6},{9,8},{10,9},{11,10},{12... | collective-permute-start | bytes 110600 | tf_op jit(solution)/shard_map/ppermute | solution.py:27
  30.7 1.1 copy.93
  31.8 2.2 %collective-permute-start.3 = (f32[1152,1,18]{0,2,1:T(8,128)S(1)}, f32[1152,1,18]{0,2,1:T(8,128)S(1)}, u32[]{:S(2)}, u32[]{:S(2)}) collective-permute-start(f32[1152,1,18]{0,2,1:T(8,128)S(1)} %get-tuple-element.19), channel_id=1, source_target_pairs={{1,0},{2,1},{3,2},{4,3},{5,4},{6,5},{7,6},{9,8},{10,9},{11,10},{12... | collective-permute-start | bytes 248840 | tf_op jit(solution)/shard_map/ppermute | solution.py:27
  34.0 3.9 %collective-permute-start.2 = (f32[1152,1,18]{0,2,1:T(8,128)S(1)}, f32[1152,1,18]{0,2,1:T(8,128)S(1)}, u32[]{:S(2)}, u32[]{:S(2)}) collective-permute-start(f32[1152,1,18]{0,2,1:T(8,128)S(1)} %get-tuple-element.18), channel_id=1, source_target_pairs={{0,1},{1,2},{2,3},{3,4},{4,5},{5,6},{6,7},{8,9},{9,10},{10,11},{11... | collective-permute-start | bytes 248840 | tf_op jit(solution)/shard_map/ppermute | solution.py:25
  38.0 0.9 fusion.55
  38.9 5.4 %collective-permute-done.2 = f32[1152,1,18]{0,2,1:T(8,128)S(1)} collective-permute-done((f32[1152,1,18]{0,2,1:T(8,128)S(1)}, f32[1152,1,18]{0,2,1:T(8,128)S(1)}, u32[]{:S(2)}, u32[]{:S(2)}) %collective-permute-start.2) | collective-permute-done | bytes 82976 | tf_op jit(solution)/shard_map/ppermute | solution.py:25
  44.3 3.6 %fusion.89 = (bf16[1152,32,16]{0,2,1:T(8,128)(2,1)S(1)}, f32[1152,32,16]{0,2,1:T(8,128)S(1)}) fusion(f32[1152,32,16]{0,2,1:T(8,128)S(1)} %copy-done.3, f32[1152,1,18]{0,2,1:T(8,128)S(1)} %collective-permute-done.3, f32[1152,32,1]{0,2,1:T(1,128)S(1)} %copy.95, f32[1152,32,1]{0,2,1:T(1,128)S(1)} %copy.93, f32[1152,1,18]{0,2,1:T(8,128)S(1)} %collective-permute-done.2, ...), kind=kLoop, calls=%fused_computation.171 | loop fusion | flops 16515072 | bytes 6374400 | tf_op jit(solution)/shard_map/convert_element_type | solution.py:88
  48.0 3.7 %fusion.5 = f32[1152,512]{0,1:T(8,128)S(1)} fusion(bf16[1152,512,1]{0,1,2:T(8,128)(2,1)S(1)} %bitcast.76, bf16[1,1,2,1152,1152]{4,3,2,1,0:T(8,128)(2,1)S(1)} %bitcast.82, f32[2,512]{1,0:T(2,128)S(1)} %compare_convert_fusion), kind=kOutput, calls=%fused_computation.7 | convolution fusion | flops 2719678464 | bytes 8851456 | tf_op jit(solution)/shard_map/mab,bp->map/dot_general | solution.py:89
  51.9 0.3 add_multiply_fusion.1
  52.2 0.5 fusion.38
  52.7 0.3 copy.155
  53.2 0.4 fusion.75
  53.6 0.5 fusion.63
  54.1 3.8 %collective-permute-start.13 = (f32[4,32,1,128]{3,1,0,2:T(8,128)S(1)}, f32[4,32,1,128]{3,1,0,2:T(8,128)S(1)}, u32[]{:S(2)}, u32[]{:S(2)}) collective-permute-start(f32[4,32,1,128]{3,1,0,2:T(8,128)S(1)} %get-tuple-element.35), channel_id=1, source_target_pairs={{8,0},{16,8},{24,16},{32,24},{40,32},{48,40},{56,48},{64,56},{72,6... | collective-permute-start | bytes 196616 | tf_op jit(solution)/shard_map/ppermute | solution.py:27
  57.9 1.9 %collective-permute-start.12 = (f32[4,32,1,128]{3,1,0,2:T(8,128)S(1)}, f32[4,32,1,128]{3,1,0,2:T(8,128)S(1)}, u32[]{:S(2)}, u32[]{:S(2)}) collective-permute-start(f32[4,32,1,128]{3,1,0,2:T(8,128)S(1)} %get-tuple-element.34), channel_id=1, source_target_pairs={{0,8},{8,16},{16,24},{24,32},{32,40},{40,48},{48,56},{56,64},{64,7... | collective-permute-start | bytes 196616 | tf_op jit(solution)/shard_map/ppermute | solution.py:25
  60.1 5.5 %collective-permute-done.12 = f32[4,32,1,128]{3,1,0,2:T(8,128)S(1)} collective-permute-done((f32[4,32,1,128]{3,1,0,2:T(8,128)S(1)}, f32[4,32,1,128]{3,1,0,2:T(8,128)S(1)}, u32[]{:S(2)}, u32[]{:S(2)}) %collective-permute-start.12) | collective-permute-done | bytes 65568 | tf_op jit(solution)/shard_map/ppermute | solution.py:25
  65.7 1.9 %collective-permute-start.14 = (f32[4,1,18,128]{3,1,0,2:T(1,128)S(1)}, f32[4,1,18,128]{3,1,0,2:T(1,128)S(1)}, u32[]{:S(2)}, u32[]{:S(2)}) collective-permute-start(f32[4,1,18,128]{3,1,0,2:T(1,128)S(1)} %get-tuple-element.31), channel_id=1, source_target_pairs={{0,1},{1,2},{2,3},{3,4},{4,5},{5,6},{6,7},{8,9},{9,10},{10,11},{11... | collective-permute-start | bytes 110600 | tf_op jit(solution)/shard_map/ppermute | solution.py:25
  67.6 7.5 %collective-permute-start.15 = (f32[4,1,18,128]{3,1,0,2:T(1,128)S(1)}, f32[4,1,18,128]{3,1,0,2:T(1,128)S(1)}, u32[]{:S(2)}, u32[]{:S(2)}) collective-permute-start(f32[4,1,18,128]{3,1,0,2:T(1,128)S(1)} %get-tuple-element.30), channel_id=1, source_target_pairs={{1,0},{2,1},{3,2},{4,3},{5,4},{6,5},{7,6},{9,8},{10,9},{11,10},{12... | collective-permute-start | bytes 110600 | tf_op jit(solution)/shard_map/ppermute | solution.py:27
  75.2 1.9 %collective-permute-start.9 = (f32[1152,32,1]{0,1,2:T(8,128)S(1)}, f32[1152,32,1]{0,1,2:T(8,128)S(1)}, u32[]{:S(2)}, u32[]{:S(2)}) collective-permute-start(f32[1152,32,1]{0,1,2:T(8,128)S(1)} %copy.117), channel_id=1, source_target_pairs={{8,0},{16,8},{24,16},{32,24},{40,32},{48,40},{56,48},{64,56},{72,6... | collective-permute-start | bytes 442376 | tf_op jit(solution)/shard_map/ppermute | solution.py:27
  77.2 2.4 %collective-permute-start.8 = (f32[1152,32,1]{0,1,2:T(8,128)S(1)}, f32[1152,32,1]{0,1,2:T(8,128)S(1)}, u32[]{:S(2)}, u32[]{:S(2)}) collective-permute-start(f32[1152,32,1]{0,1,2:T(8,128)S(1)} %copy.115), channel_id=1, source_target_pairs={{0,8},{8,16},{16,24},{24,32},{32,40},{40,48},{48,56},{56,64},{64,7... | collective-permute-start | bytes 442376 | tf_op jit(solution)/shard_map/ppermute | solution.py:25
  80.2 0.3 maximum_maximum_fusion
  80.7 5.2 %collective-permute-done.8 = f32[1152,32,1]{0,1,2:T(8,128)S(1)} collective-permute-done((f32[1152,32,1]{0,1,2:T(8,128)S(1)}, f32[1152,32,1]{0,1,2:T(8,128)S(1)}, u32[]{:S(2)}, u32[]{:S(2)}) %collective-permute-start.8) | collective-permute-done | bytes 147488 | tf_op jit(solution)/shard_map/ppermute | solution.py:25
  86.1 2.2 %collective-permute-start.11 = (f32[1152,1,18]{0,2,1:T(8,128)S(1)}, f32[1152,1,18]{0,2,1:T(8,128)S(1)}, u32[]{:S(2)}, u32[]{:S(2)}) collective-permute-start(f32[1152,1,18]{0,2,1:T(8,128)S(1)} %get-tuple-element.17), channel_id=1, source_target_pairs={{1,0},{2,1},{3,2},{4,3},{5,4},{6,5},{7,6},{9,8},{10,9},{11,10},{12... | collective-permute-start | bytes 248840 | tf_op jit(solution)/shard_map/ppermute | solution.py:27
  88.3 4.1 %collective-permute-start.10 = (f32[1152,1,18]{0,2,1:T(8,128)S(1)}, f32[1152,1,18]{0,2,1:T(8,128)S(1)}, u32[]{:S(2)}, u32[]{:S(2)}) collective-permute-start(f32[1152,1,18]{0,2,1:T(8,128)S(1)} %get-tuple-element.16), channel_id=1, source_target_pairs={{0,1},{1,2},{2,3},{3,4},{4,5},{5,6},{6,7},{8,9},{9,10},{10,11},{11... | collective-permute-start | bytes 248840 | tf_op jit(solution)/shard_map/ppermute | solution.py:25
  92.4 0.6 fusion.46
  93.0 5.5 %collective-permute-done.10 = f32[1152,1,18]{0,2,1:T(8,128)S(1)} collective-permute-done((f32[1152,1,18]{0,2,1:T(8,128)S(1)}, f32[1152,1,18]{0,2,1:T(8,128)S(1)}, u32[]{:S(2)}, u32[]{:S(2)}) %collective-permute-start.10) | collective-permute-done | bytes 82976 | tf_op jit(solution)/shard_map/ppermute | solution.py:25
  98.5 3.6 %fusion.87 = (bf16[1152,32,16]{0,2,1:T(8,128)(2,1)S(1)}, f32[1152,32,16]{0,2,1:T(8,128)S(1)}) fusion(f32[1152,32,16]{0,2,1:T(8,128)S(1)} %copy-done.2, f32[1152,1,18]{0,2,1:T(8,128)S(1)} %collective-permute-done.11, f32[1152,32,1]{0,2,1:T(1,128)S(1)} %copy.118, f32[1152,32,1]{0,2,1:T(1,128)S(1)} %copy.116, f32[1152,1,18]{0,2,1:T(8,128)S(1)} %collective-permute-done.10, ...), kind=kLoop, calls=%fused_computation.170 | loop fusion | flops 16515072 | bytes 6374400 | tf_op jit(solution)/shard_map/convert_element_type | solution.py:88
  102.2 3.7 %fusion.4 = f32[1152,512]{0,1:T(8,128)S(1)} fusion(bf16[1152,512,1]{0,1,2:T(8,128)(2,1)S(1)} %bitcast.75, bf16[1,1,2,1152,1152]{4,3,2,1,0:T(8,128)(2,1)S(1)} %bitcast.84, f32[2,512]{1,0:T(2,128)S(1)} %compare_convert_fusion), kind=kOutput, calls=%fused_computation.5 | convolution fusion | flops 2719678464 | bytes 8851456 | tf_op jit(solution)/shard_map/mab,bp->map/dot_general | solution.py:89
  106.1 0.3 add_multiply_fusion
  106.4 0.5 fusion.36
  106.9 0.3 copy.154
  107.4 0.4 copy-done.4
  107.8 0.3 fusion.68
  108.1 0.3 fusion.64
  108.4 1.6 %copy.124 = f32[4,32,16,128]{3,2,1,0:T(8,128)} copy(f32[4,32,16,128]{3,1,0,2:T(8,128)S(1)} %fusion.64) | data formatting | bytes 2097152
  (66 shorter events, 2.9 us)
Async XLA Ops:
  0.6 51.6 %copy-start = (bf16[1152,256]{1,0:T(8,128)(2,1)S(1)}, bf16[1152,256]{1,0:T(8,128)(2,1)}, u32[]{:S(2)}) copy-start(bf16[1152,256]{1,0:T(8,128)(2,1)} %param.12) | copy-start | bytes 1769476
  2.5 15.7 %copy-start.8 = (s32[32,16]{0,1:T(8,128)S(1)}, s32[32,16]{0,1:T(8,128)}, u32[]{:S(2)}) copy-start(s32[32,16]{0,1:T(8,128)} %param.10) | copy-start | bytes 6148
  2.6 15.8 %copy-start.7 = (s32[32,16]{0,1:T(8,128)S(1)}, s32[32,16]{0,1:T(8,128)}, u32[]{:S(2)}) copy-start(s32[32,16]{0,1:T(8,128)} %param.9) | copy-start | bytes 6148
  2.6 15.9 %copy-start.6 = (f32[2,1152]{1,0:T(2,128)S(1)}, f32[2,1152]{1,0:T(2,128)}, u32[]{:S(2)}) copy-start(f32[2,1152]{1,0:T(2,128)} %param.11) | copy-start | bytes 27652
  2.6 16.8 %copy-start.5 = (f32[4,32,16,128]{3,2,1,0:T(8,128)S(1)}, f32[4,32,16,128]{3,2,1,0:T(8,128)}, u32[]{:S(2)}) copy-start(f32[4,32,16,128]{3,2,1,0:T(8,128)} %param.13) | copy-start | bytes 3145732
  2.6 27.9 %collective-permute-start.1 = (f32[1152,32,1]{0,1,2:T(8,128)S(1)}, f32[1152,32,1]{0,1,2:T(8,128)S(1)}, u32[]{:S(2)}, u32[]{:S(2)}) collective-permute-start(f32[1152,32,1]{0,1,2:T(8,128)S(1)} %copy.138), channel_id=1, source_target_pairs={{8,0},{16,8},{24,16},{32,24},{40,32},{48,40},{56,48},{64,56},{72,6... | collective-permute-start | bytes 442376 | tf_op jit(solution)/shard_map/ppermute | solution.py:27
  5.5 25.2 %collective-permute-start = (f32[1152,32,1]{0,1,2:T(8,128)}, f32[1152,32,1]{0,1,2:T(8,128)}, u32[]{:S(2)}, u32[]{:S(2)}) collective-permute-start(f32[1152,32,1]{0,1,2:T(8,128)} %copy.137), channel_id=1, source_target_pairs={{0,8},{8,16},{16,24},{24,32},{32,40},{40,48},{48,56},{56,64},{64,7... | collective-permute-start | bytes 442376 | tf_op jit(solution)/shard_map/ppermute | solution.py:25
  10.0 8.6 %collective-permute-start.4 = (f32[4,32,1,128]{3,1,0,2:T(8,128)}, f32[4,32,1,128]{3,1,0,2:T(8,128)}, u32[]{:S(2)}, u32[]{:S(2)}) collective-permute-start(f32[4,32,1,128]{3,1,0,2:T(8,128)} %get-tuple-element.42), channel_id=1, source_target_pairs={{0,8},{8,16},{16,24},{24,32},{32,40},{40,48},{48,56},{56,64},{64,7... | collective-permute-start | bytes 196616 | tf_op jit(solution)/shard_map/ppermute | solution.py:25
  12.9 7.0 %collective-permute-start.5 = (f32[4,32,1,128]{3,1,0,2:T(8,128)}, f32[4,32,1,128]{3,1,0,2:T(8,128)}, u32[]{:S(2)}, u32[]{:S(2)}) collective-permute-start(f32[4,32,1,128]{3,1,0,2:T(8,128)} %get-tuple-element.41), channel_id=1, source_target_pairs={{8,0},{16,8},{24,16},{32,24},{40,32},{48,40},{56,48},{64,56},{72,6... | collective-permute-start | bytes 196616 | tf_op jit(solution)/shard_map/ppermute | solution.py:27
  19.4 12.3 %copy-start.3 = (f32[1152,32,16]{0,2,1:T(8,128)S(1)}, f32[1152,32,16]{0,2,1:T(8,128)}, u32[]{:S(2)}) copy-start(f32[1152,32,16]{0,2,1:T(8,128)} %param.7) | copy-start | bytes 7077892
  21.1 16.9 %collective-permute-start.6 = (f32[4,1,18,128]{3,1,0,2:T(1,128)S(1)}, f32[4,1,18,128]{3,1,0,2:T(1,128)S(1)}, u32[]{:S(2)}, u32[]{:S(2)}) collective-permute-start(f32[4,1,18,128]{3,1,0,2:T(1,128)S(1)} %get-tuple-element.33), channel_id=1, source_target_pairs={{0,1},{1,2},{2,3},{3,4},{4,5},{5,6},{6,7},{8,9},{9,10},{10,11},{11... | collective-permute-start | bytes 110600 | tf_op jit(solution)/shard_map/ppermute | solution.py:25
  24.6 13.4 %collective-permute-start.7 = (f32[4,1,18,128]{3,1,0,2:T(1,128)S(1)}, f32[4,1,18,128]{3,1,0,2:T(1,128)S(1)}, u32[]{:S(2)}, u32[]{:S(2)}) collective-permute-start(f32[4,1,18,128]{3,1,0,2:T(1,128)S(1)} %get-tuple-element.32), channel_id=1, source_target_pairs={{1,0},{2,1},{3,2},{4,3},{5,4},{6,5},{7,6},{9,8},{10,9},{11,10},{12... | collective-permute-start | bytes 110600 | tf_op jit(solution)/shard_map/ppermute | solution.py:27
  31.8 16.1 %slice-start = ((s8[5308416]{0:T(1024)(128)(4,1)}), s8[4194304]{0:T(1024)(128)(4,1)S(1)}, s32[]{:S(2)}) async-start(s8[5308416]{0:T(1024)(128)(4,1)} %bitcast.81), calls=%async_computation | async-start | bytes 8388608
  31.8 7.1 %collective-permute-start.3 = (f32[1152,1,18]{0,2,1:T(8,128)S(1)}, f32[1152,1,18]{0,2,1:T(8,128)S(1)}, u32[]{:S(2)}, u32[]{:S(2)}) collective-permute-start(f32[1152,1,18]{0,2,1:T(8,128)S(1)} %get-tuple-element.19), channel_id=1, source_target_pairs={{1,0},{2,1},{3,2},{4,3},{5,4},{6,5},{7,6},{9,8},{10,9},{11,10},{12... | collective-permute-start | bytes 248840 | tf_op jit(solution)/shard_map/ppermute | solution.py:27
  34.0 10.3 %collective-permute-start.2 = (f32[1152,1,18]{0,2,1:T(8,128)S(1)}, f32[1152,1,18]{0,2,1:T(8,128)S(1)}, u32[]{:S(2)}, u32[]{:S(2)}) collective-permute-start(f32[1152,1,18]{0,2,1:T(8,128)S(1)} %get-tuple-element.18), channel_id=1, source_target_pairs={{0,1},{1,2},{2,3},{3,4},{4,5},{5,6},{6,7},{8,9},{9,10},{10,11},{11... | collective-permute-start | bytes 248840 | tf_op jit(solution)/shard_map/ppermute | solution.py:25
  38.0 10.0 %slice-start.1 = ((s8[5308416]{0:T(1024)(128)(4,1)}), s8[1114112]{0:T(1024)(128)(4,1)S(1)}, s32[]{:S(2)}) async-start(s8[5308416]{0:T(1024)(128)(4,1)} %bitcast.81), calls=%async_computation.1 | async-start | bytes 2228224
  52.2 7.7 %copy-start.1 = (f32[1152,32,16]{0,2,1:T(8,128)}, f32[1152,32,16]{0,2,1:T(8,128)S(1)}, u32[]{:S(2)}) copy-start(f32[1152,32,16]{0,2,1:T(8,128)S(1)} %add_multiply_fusion.1) | copy-start | bytes 7077892
  54.1 5.9 %collective-permute-start.13 = (f32[4,32,1,128]{3,1,0,2:T(8,128)S(1)}, f32[4,32,1,128]{3,1,0,2:T(8,128)S(1)}, u32[]{:S(2)}, u32[]{:S(2)}) collective-permute-start(f32[4,32,1,128]{3,1,0,2:T(8,128)S(1)} %get-tuple-element.35), channel_id=1, source_target_pairs={{8,0},{16,8},{24,16},{32,24},{40,32},{48,40},{56,48},{64,56},{72,6... | collective-permute-start | bytes 196616 | tf_op jit(solution)/shard_map/ppermute | solution.py:27
  57.9 7.7 %collective-permute-start.12 = (f32[4,32,1,128]{3,1,0,2:T(8,128)S(1)}, f32[4,32,1,128]{3,1,0,2:T(8,128)S(1)}, u32[]{:S(2)}, u32[]{:S(2)}) collective-permute-start(f32[4,32,1,128]{3,1,0,2:T(8,128)S(1)} %get-tuple-element.34), channel_id=1, source_target_pairs={{0,8},{8,16},{16,24},{24,32},{32,40},{40,48},{48,56},{56,64},{64,7... | collective-permute-start | bytes 196616 | tf_op jit(solution)/shard_map/ppermute | solution.py:25
  65.7 14.5 %collective-permute-start.14 = (f32[4,1,18,128]{3,1,0,2:T(1,128)S(1)}, f32[4,1,18,128]{3,1,0,2:T(1,128)S(1)}, u32[]{:S(2)}, u32[]{:S(2)}) collective-permute-start(f32[4,1,18,128]{3,1,0,2:T(1,128)S(1)} %get-tuple-element.31), channel_id=1, source_target_pairs={{0,1},{1,2},{2,3},{3,4},{4,5},{5,6},{6,7},{8,9},{9,10},{10,11},{11... | collective-permute-start | bytes 110600 | tf_op jit(solution)/shard_map/ppermute | solution.py:25
  67.6 12.6 %collective-permute-start.15 = (f32[4,1,18,128]{3,1,0,2:T(1,128)S(1)}, f32[4,1,18,128]{3,1,0,2:T(1,128)S(1)}, u32[]{:S(2)}, u32[]{:S(2)}) collective-permute-start(f32[4,1,18,128]{3,1,0,2:T(1,128)S(1)} %get-tuple-element.30), channel_id=1, source_target_pairs={{1,0},{2,1},{3,2},{4,3},{5,4},{6,5},{7,6},{9,8},{10,9},{11,10},{12... | collective-permute-start | bytes 110600 | tf_op jit(solution)/shard_map/ppermute | solution.py:27
  75.2 5.3 %collective-permute-start.9 = (f32[1152,32,1]{0,1,2:T(8,128)S(1)}, f32[1152,32,1]{0,1,2:T(8,128)S(1)}, u32[]{:S(2)}, u32[]{:S(2)}) collective-permute-start(f32[1152,32,1]{0,1,2:T(8,128)S(1)} %copy.117), channel_id=1, source_target_pairs={{8,0},{16,8},{24,16},{32,24},{40,32},{48,40},{56,48},{64,56},{72,6... | collective-permute-start | bytes 442376 | tf_op jit(solution)/shard_map/ppermute | solution.py:27
  77.2 8.7 %collective-permute-start.8 = (f32[1152,32,1]{0,1,2:T(8,128)S(1)}, f32[1152,32,1]{0,1,2:T(8,128)S(1)}, u32[]{:S(2)}, u32[]{:S(2)}) collective-permute-start(f32[1152,32,1]{0,1,2:T(8,128)S(1)} %copy.115), channel_id=1, source_target_pairs={{0,8},{8,16},{16,24},{24,32},{32,40},{40,48},{48,56},{56,64},{64,7... | collective-permute-start | bytes 442376 | tf_op jit(solution)/shard_map/ppermute | solution.py:25
  80.1 5.9 %copy-start.2 = (f32[1152,32,16]{0,2,1:T(8,128)S(1)}, f32[1152,32,16]{0,2,1:T(8,128)}, u32[]{:S(2)}) copy-start(f32[1152,32,16]{0,2,1:T(8,128)} %copy-done.1) | copy-start | bytes 7077892
  86.0 16.1 %slice-start.2 = ((s8[5308416]{0:T(1024)(128)(4,1)}), s8[4194304]{0:T(1024)(128)(4,1)S(1)}, s32[]{:S(2)}) async-start(s8[5308416]{0:T(1024)(128)(4,1)} %bitcast.83), calls=%async_computation.2 | async-start | bytes 8388608
  86.1 6.9 %collective-permute-start.11 = (f32[1152,1,18]{0,2,1:T(8,128)S(1)}, f32[1152,1,18]{0,2,1:T(8,128)S(1)}, u32[]{:S(2)}, u32[]{:S(2)}) collective-permute-start(f32[1152,1,18]{0,2,1:T(8,128)S(1)} %get-tuple-element.17), channel_id=1, source_target_pairs={{1,0},{2,1},{3,2},{4,3},{5,4},{6,5},{7,6},{9,8},{10,9},{11,10},{12... | collective-permute-start | bytes 248840 | tf_op jit(solution)/shard_map/ppermute | solution.py:27
  88.3 10.3 %collective-permute-start.10 = (f32[1152,1,18]{0,2,1:T(8,128)S(1)}, f32[1152,1,18]{0,2,1:T(8,128)S(1)}, u32[]{:S(2)}, u32[]{:S(2)}) collective-permute-start(f32[1152,1,18]{0,2,1:T(8,128)S(1)} %get-tuple-element.16), channel_id=1, source_target_pairs={{0,1},{1,2},{2,3},{3,4},{4,5},{5,6},{6,7},{8,9},{9,10},{10,11},{11... | collective-permute-start | bytes 248840 | tf_op jit(solution)/shard_map/ppermute | solution.py:25
  92.4 9.8 %slice-start.3 = ((s8[5308416]{0:T(1024)(128)(4,1)}), s8[1114112]{0:T(1024)(128)(4,1)S(1)}, s32[]{:S(2)}) async-start(s8[5308416]{0:T(1024)(128)(4,1)} %bitcast.83), calls=%async_computation.3 | async-start | bytes 2228224
  106.4 1.4 %copy-start.4 = (f32[1152,32,16]{0,2,1:T(8,128)}, f32[1152,32,16]{0,2,1:T(8,128)S(1)}, u32[]{:S(2)}) copy-start(f32[1152,32,16]{0,2,1:T(8,128)S(1)} %add_multiply_fusion) | copy-start | bytes 7077892
where the time goes:
time: 111 us; the launch traced here: 110 us
  starting transfers between devices  53.4 us (48%)
  waiting for transfers between devices  21.6 us (19%)
  local copies, waits for them, and re-layouts  13 us (12%)
  other arithmetic  12.2 us (11%)
  matrix products  8.47 us (8%)
  between operations  1.29 us (1%)
    ppermute x8, starting transfers between devices, with_halo(): lax.ppermute(head, axis, [((i + 1) % count, i) for i in range(ends)])  30.5 us
    ppermute x8, starting transfers between devices, with_halo(): lax.ppermute(tail, axis, [(i, (i + 1) % count) for i in range(ends)])  23 us
    ppermute x8, waiting for transfers between devices, with_halo(): lax.ppermute(tail, axis, [(i, (i + 1) % count) for i in range(ends)])  21.6 us
    dot_general x2, matrix products, local(): jnp.einsum('mab,bp->map', matrix_set, flattened, preferred_element_type=j...  7.45 us
    convert_element_type x2, other arithmetic, local(): advected.astype(jnp.bfloat16).reshape(bins_all, block_rows * block_cols)  7.27 us
    unnamed x33, local copies, waits for them, and re-layouts  5.69 us
  transfers between devices with their start and end apart: 16, of which 4 were waited for; matrix products, arithmetic and copies ran while one was open for 9% of the time, Pallas kernels for 0%

commit v1 on v0

v1 whole, which is shorter than its diff:
```python
import functools
import jax
import jax.numpy as jnp
from jax import lax
from jax.sharding import PartitionSpec as P
from jax.experimental import pallas as pl
from jax.experimental.pallas import tpu as pltpu

STEPS = 2
current_gain = 0.2
source_gain = 0.5
mixing_side = 0.15
mixing_depth = 0.2
rotation = 0.3
transport = 0.5

LANES = 128
PITCH = 24
LEAD = 8
W, E, N, S = range(4)


def kernel(rows, cols, tiles, mats_count,
           e0, mats, own_h, mask_h, cour_h, stok_h, oc,
           e_out, o_out,
           ebuf, xbuf, low, elow, mbuf, stok, cour, ownv, maskv, obuf,
           sea, o0, o1, ux, uy, drift,
           epack, ehx, ehy, opack, ohx, ohy,
           lsem, esem, ersem, osem, orsem, wsem):
    g = lax.axis_index("grp")
    t = lax.axis_index("tile")
    ng = lax.axis_size("grp")
    nt = lax.axis_size("tile")
    bins = tiles * LANES
    points = rows * cols
    has = [g > 0, g < ng - 1, t > 0, t < nt - 1]
    peer = [{"grp": g - 1}, {"grp": g + 1}, {"tile": t - 1}, {"tile": t + 1}]
    back = [E, W, S, N]
    chunks = [(k, min(2, tiles - k)) for k in range(0, tiles, 2)]
    fields = obuf.shape[1]

    e4 = ebuf.reshape(tiles, rows + 2, PITCH, LANES)
    o5 = obuf.reshape(2, fields, rows + 2, PITCH, LANES)

    loads = []

    def load(src, dst):
        copy = pltpu.make_async_copy(src, dst, lsem.at[len(loads)])
        copy.start()
        loads.append(copy)
        return copy

    e_load = [load(e0.at[:, :, pl.ds(k * LANES, LANES)], e4.at[k, pl.ds(1, rows), pl.ds(LEAD, cols), :]) for k in range(tiles)]
    small = [load(oc, o5.at[0, :, pl.ds(1, rows), pl.ds(LEAD, cols), :]),
             load(cour_h, cour), load(mask_h, maskv), load(own_h, ownv)]
    m_load = []
    for k, width in chunks:
        span = pl.ds(k * LANES, width * LANES)
        m_load.append([load(mats.at[m, span, :], mbuf.at[span, pl.ds(m * bins, bins)]) for m in range(mats_count)])
    stok_load = load(stok_h, stok)

    barrier = pltpu.get_barrier_semaphore()
    for d in range(4):
        @pl.when(has[d])
        def _(d=d):
            pl.semaphore_signal(barrier, inc=1, device_id=peer[d], device_id_type=pl.DeviceIdType.MESH)

    for d in range(4):
        @pl.when(jnp.logical_not(has[d]))
        def _(d=d):
            if d < 2:
                ehx[:, d] = jnp.zeros_like(ehx[:, d])
                ohx[:, d] = jnp.zeros_like(ohx[:, d])
            else:
                ehy[:, d - 2] = jnp.zeros_like(ehy[:, d - 2])
                ohy[:, d - 2] = jnp.zeros_like(ohy[:, d - 2])

    def e_copy(step, d, c):
        k, width = chunks[c]
        span = pl.ds(k, width)
        far = back[d]
        if d < 2:
            src = epack.at[step, d, span]
            dst = ehx.at[step, far, span]
        else:
            src = e4.at[span, 1 if d == N else rows, pl.ds(LEAD, cols), :]
            dst = ehy.at[step, far - 2, span]
        return pltpu.make_async_remote_copy(
            src_ref=src, dst_ref=dst, send_sem=esem.at[step, d, c], recv_sem=ersem.at[step, far, c],
            device_id=peer[d], device_id_type=pl.DeviceIdType.MESH)

    def e_arrival(step, side, c):
        k, width = chunks[c]
        span = pl.ds(k, width)
        dst = ehx.at[step, side, span] if side < 2 else ehy.at[step, side - 2, span]
        return pltpu.make_async_remote_copy(
            src_ref=dst, dst_ref=dst, send_sem=esem.at[step, side, c], recv_sem=ersem.at[step, side, c],
            device_id=peer[side], device_id_type=pl.DeviceIdType.MESH)

    def o_copy(step, d):
        far = back[d]
        if d < 2:
            src = opack.at[step, d]
            dst = ohx.at[step, far]
        else:
            src = o5.at[step, :, 1 if d == N else rows, pl.ds(LEAD, cols), :]
            dst = ohy.at[step, far - 2]
        return pltpu.make_async_remote_copy(
            src_ref=src, dst_ref=dst, send_sem=osem.at[step, d], recv_sem=orsem.at[step, far],
            device_id=peer[d], device_id_type=pl.DeviceIdType.MESH)

    def o_arrival(step, side):
        dst = ohx.at[step, side] if side < 2 else ohy.at[step, side - 2]
        return pltpu.make_async_remote_copy(
            src_ref=dst, dst_ref=dst, send_sem=osem.at[step, side], recv_sem=orsem.at[step, side],
            device_id=peer[side], device_id_type=pl.DeviceIdType.MESH)

    first_col = pl.ds(PITCH + LEAD, rows, stride=PITCH)
    last_col = pl.ds(PITCH + LEAD + cols - 1, rows, stride=PITCH)
    west_col = pl.ds(PITCH + LEAD - 1, rows, stride=PITCH)
    east_col = pl.ds(PITCH + LEAD + cols, rows, stride=PITCH)

    def e_pack(step, c):
        k0, width = chunks[c]
        for k in range(k0, k0 + width):
            epack[step, W, k] = ebuf[k, first_col, :]
            epack[step, E, k] = ebuf[k, last_col, :]

    def o_pack(step):
        for q in range(fields):
            opack[step, W, q] = obuf[step, q, first_col, :]
            opack[step, E, q] = obuf[step, q, last_col, :]

    def send(make):
        for d in range(4):
            @pl.when(has[d])
            def _(d=d):
                make(d).start()

    def wait_recv(make):
        for d in range(4):
            @pl.when(has[d])
            def _(d=d):
                make(d).wait_recv()

    def wait_send(make):
        for d in range(4):
            @pl.when(has[d])
            def _(d=d):
                make(d).wait_send()

    for c, (k0, width) in enumerate(chunks):
        for k in range(k0, k0 + width):
            e_load[k].wait()
        e_pack(0, c)
        if c == 0:
            pl.semaphore_wait(barrier, sum(h.astype(jnp.int32) for h in has))
        send(lambda d: e_copy(0, d, c))
    for copy in small:
        copy.wait()
    o_pack(0)
    send(lambda d: o_copy(0, d))

    mask_all = maskv[...].astype(jnp.float32)
    own_all = ownv[...]
    own0 = jnp.where(own_all == 0, 1.0, 0.0)
    own1 = jnp.where(own_all == 1, 1.0, 0.0)
    for r in range(rows):
        at = pl.ds(r * cols, cols)
        sea[at, :] = jnp.broadcast_to(mask_all[:, r:r + 1], (cols, LANES))
        o0[at, :] = jnp.broadcast_to(own0[:, r:r + 1], (cols, LANES))
        o1[at, :] = jnp.broadcast_to(own1[:, r:r + 1], (cols, LANES))
        for q, dst in ((0, ux), (1, uy)):
            here = obuf[0, q, pl.ds((r + 1) * PITCH + LEAD, cols), :]
            dst[at, :] = current_gain * jnp.broadcast_to(here[:, 0:1], (cols, LANES))

    def advect(step, k):
        cx = jnp.broadcast_to(cour[0:1, k * LANES:(k + 1) * LANES], (cols, LANES))
        cy = jnp.broadcast_to(cour[1:2, k * LANES:(k + 1) * LANES], (cols, LANES))

        @pl.loop(0, rows // 8)
        def _(block):
            for i in range(8):
                r = block * 8 + i
                base = (r + 1) * PITCH + LEAD
                at = pl.ds(pl.multiple_of(r * cols, cols), cols)
                mid = ebuf[k, pl.ds(base, cols), :]
                west = ebuf[k, pl.ds(base - 1, cols), :]
                east = ebuf[k, pl.ds(base + 1, cols), :]
                north = ebuf[k, pl.ds(base - PITCH, cols), :]
                south = ebuf[k, pl.ds(base + PITCH, cols), :]
                sx = cx + ux[at, :]
                sy = cy + uy[at, :]
                flux = sx * jnp.where(sx > 0.0, mid - west, east - mid)
                flux = flux + sy * jnp.where(sy > 0.0, mid - north, south - mid)
                adv = sea[at, :] * (mid - flux)
                xbuf[k, at, :] = adv
                low[at, k * LANES:(k + 1) * LANES] = (adv * o0[at, :]).astype(jnp.bfloat16)
                low[at, bins + k * LANES:bins + (k + 1) * LANES] = (adv * o1[at, :]).astype(jnp.bfloat16)

    lane = lax.broadcasted_iota(jnp.int32, (cols, LANES), 1)

    def ocean(step):
        dst_o = 1 - step

        @pl.loop(0, rows)
        def _(r):
            base = (r + 1) * PITCH + LEAD
            at = pl.ds(pl.multiple_of(r * cols, cols), cols)
            d0 = drift[at, 0:LANES]
            d1 = drift[at, LANES:2 * LANES]
            sm = sea[at, :]
            mids = [obuf[step, q, pl.ds(base, cols), :] for q in range(fields)]
            for q in range(fields):
                mid = mids[q]
                west = obuf[step, q, pl.ds(base - 1, cols), :]
                east = obuf[step, q, pl.ds(base + 1, cols), :]
                north = obuf[step, q, pl.ds(base - PITCH, cols), :]
                south = obuf[step, q, pl.ds(base + PITCH, cols), :]
                above = jnp.where(lane == LANES - 1, 0.0, pltpu.roll(mid, LANES - 1, 1))
                below = jnp.where(lane == 0, 0.0, pltpu.roll(mid, 1, 1))
                mix = mixing_side * (north + south + west + east - 4.0 * mid) + mixing_depth * (above + below - 2.0 * mid)
                if q == 0:
                    tend = mix + rotation * (mids[1] + d1)
                elif q == 1:
                    tend = mix - rotation * (mids[0] + d0)
                else:
                    tend = mix - transport * (d0 * (0.5 * (east - west)) + d1 * (0.5 * (south - north)))
                new = mid + sm * tend
                obuf[dst_o, q, pl.ds(base, cols), :] = new
                if step == 0 and q < 2:
                    dst = (ux, uy)[q]
                    dst[at, :] = current_gain * jnp.broadcast_to(new[:, 0:1], (cols, LANES))

    out_copies = []
    for step in range(STEPS):
        for c, (k0, width) in enumerate(chunks):
            wait_recv(lambda d: e_arrival(step, d, c))
            for k in range(k0, k0 + width):
                ebuf[k, west_col, :] = ehx[step, W, k]
                ebuf[k, east_col, :] = ehx[step, E, k]
                ebuf[k, pl.ds(LEAD, cols), :] = ehy[step, 0, k]
                ebuf[k, pl.ds((rows + 1) * PITCH + LEAD, cols), :] = ehy[step, 1, k]
                advect(step, k)
        for c in range(len(chunks)):
            wait_send(lambda d: e_copy(step, d, c))
        for c, (k0, width) in enumerate(chunks):
            if step == 0:
                for copy in m_load[c]:
                    copy.wait()
            src = lax.dot_general(
                low[...], mbuf[k0 * LANES:(k0 + width) * LANES, :], (((1,), (1,)), ((), ())),
                preferred_element_type=jnp.float32)
            for k in range(k0, k0 + width):
                part = src[:, (k - k0) * LANES:(k - k0 + 1) * LANES]
                new = sea[...] * (xbuf[k] + source_gain * part)
                e4[k, 1:rows + 1, LEAD:LEAD + cols, :] = new.reshape(rows, cols, LANES)
                elow[:, k * LANES:(k + 1) * LANES] = new.astype(jnp.bfloat16)
            if step + 1 < STEPS:
                e_pack(step + 1, c)
                send(lambda d: e_copy(step + 1, d, c))
            else:
                for k in range(k0, k0 + width):
                    copy = pltpu.make_async_copy(
                        e4.at[k, pl.ds(1, rows), pl.ds(LEAD, cols), :], e_out.at[:, :, pl.ds(k * LANES, LANES)], wsem.at[k])
                    copy.start()
                    out_copies.append(copy)
        if step == 0:
            stok_load.wait()
        drift[...] = jnp.dot(elow[...], stok[...], preferred_element_type=jnp.float32)
        wait_recv(lambda d: o_arrival(step, d))
        for q in range(fields):
            obuf[step, q, west_col, :] = ohx[step, W, q]
            obuf[step, q, east_col, :] = ohx[step, E, q]
            obuf[step, q, pl.ds(LEAD, cols), :] = ohy[step, 0, q]
            obuf[step, q, pl.ds((rows + 1) * PITCH + LEAD, cols), :] = ohy[step, 1, q]
        if step == 1:
            wait_send(lambda d: o_copy(0, d))
        ocean(step)
        if step + 1 < STEPS:
            o_pack(step + 1)
            send(lambda d: o_copy(step + 1, d))
    copy = pltpu.make_async_copy(
        o5.at[0, :, pl.ds(1, rows), pl.ds(LEAD, cols), :], o_out, wsem.at[tiles])
    copy.start()
    out_copies.append(copy)
    wait_send(lambda d: o_copy(1, d))
    for copy in out_copies:
        copy.wait()


def local(spectrum, matrices, ownership, land_mask, courant, stokes_weight, ocean):
    bins, rows, cols = spectrum.shape
    mats = matrices.reshape(matrices.shape[2:])
    count = mats.shape[0]
    tiles = bins // LANES
    points = rows * cols
    fields = ocean.shape[0]
    chunk_count = -(-tiles // 2)
    flat = (rows + 2) * PITCH
    e0 = jnp.transpose(spectrum, (1, 2, 0))
    f32 = jnp.float32
    any_spec = pl.BlockSpec(memory_space=pltpu.HBM)
    e_new, o_new = pl.pallas_call(
        functools.partial(kernel, rows, cols, tiles, count),
        out_shape=(jax.ShapeDtypeStruct((rows, cols, bins), f32), jax.ShapeDtypeStruct(ocean.shape, f32)),
        in_specs=[any_spec] * 7,
        out_specs=(any_spec, any_spec),
        scratch_shapes=[
            pltpu.VMEM((tiles, flat, LANES), f32),
            pltpu.VMEM((tiles, points, LANES), f32),
            pltpu.VMEM((points, count * bins), jnp.bfloat16),
            pltpu.VMEM((points, bins), jnp.bfloat16),
            pltpu.VMEM((bins, count * bins), jnp.bfloat16),
            pltpu.VMEM((bins, 2 * LANES), jnp.bfloat16),
            pltpu.VMEM((2, bins), f32),
            pltpu.VMEM((cols, rows), jnp.int32),
            pltpu.VMEM((cols, rows), jnp.int32),
            pltpu.VMEM((2, fields, flat, LANES), f32),
        ] + [pltpu.VMEM((points, LANES), f32)] * 5 + [
            pltpu.VMEM((points, 2 * LANES), f32),
            pltpu.VMEM((STEPS, 2, tiles, rows, LANES), f32),
            pltpu.VMEM((STEPS, 2, tiles, rows, LANES), f32),
            pltpu.VMEM((STEPS, 2, tiles, cols, LANES), f32),
            pltpu.VMEM((STEPS, 2, fields, rows, LANES), f32),
            pltpu.VMEM((STEPS, 2, fields, rows, LANES), f32),
            pltpu.VMEM((STEPS, 2, fields, cols, LANES), f32),
            pltpu.SemaphoreType.DMA((tiles + 5 + chunk_count * count,)),
            pltpu.SemaphoreType.DMA((STEPS, 4, chunk_count)),
            pltpu.SemaphoreType.DMA((STEPS, 4, chunk_count)),
            pltpu.SemaphoreType.DMA((STEPS, 4)),
            pltpu.SemaphoreType.DMA((STEPS, 4)),
            pltpu.SemaphoreType.DMA((tiles + 1,)),
        ],
        compiler_params=pltpu.CompilerParams(
            collective_id=0, has_side_effects=True, vmem_limit_bytes=56 * 1024 * 1024),
    )(e0, mats, ownership.T, land_mask.T, courant, stokes_weight, ocean)
    return jnp.transpose(e_new, (2, 0, 1)), o_new


def solution(mesh):
    in_specs = (
        P(None, "tile", "grp"),
        P("tile", "grp", None, None, None),
        P("tile", "grp"),
        P("tile", "grp"),
        P(),
        P(),
        P(None, "tile", "grp", None),
    )
    out_specs = (P(None, "tile", "grp"), P(None, "tile", "grp", None))
    return jax.shard_map(local, mesh=mesh, in_specs=in_specs, out_specs=out_specs, check_vma=False)
```

time: 111 us -> 45.4 us (0.41)
  the two profiles are of different devices: /device:TPU:132 before, /device:TPU:166 now
where the time goes in v1:
time: 45.4 us; the launch traced here: 45.1 us
  Pallas kernels  40.2 us (89%)
  local copies, waits for them, and re-layouts  4.28 us (9%)
  between operations  0.65 us (1%)
    pallas_call x1, Pallas kernels, local(): pl.pallas_call(functools.partial(kernel, rows, cols, tiles, count), out_s...  40.2 us
    unnamed x4, local copies, waits for them, and re-layouts  4.28 us

profile of v1, /device:TPU:166, one launch (start us, length us, event | category | flops | bytes accessed | tf_op | source)
XLA Modules:
  0.0 45.1 jit_solution(6855266149063394291)
XLA Ops:
  0.6 40.2 %shard_map.86 = (f32[32,16,1152]{2,1,0:T(8,128)}, f32[4,32,16,128]{3,2,1,0:T(8,128)}) custom-call(f32[32,16,1152]{2,1,0:T(8,128)} %bitcast.7, bf16[2,1152,1152]{2,1,0:T(8,128)(2,1)} %bitcast.5, s32[16,32]{1,0:T(8,128)} %bitcast.8, s32[16,32]{1,0:T(8,128)} %bitcast.9, f32[2,1152]{1,0:T(2,128)} %cour_h.1, bf16[1152,256]{1,0:T(8,128)(2,1)} %stok_h.1, ...), custom_call_target="tpu_custom_call" | custom-call | tf_op jit(solution)/shard_map/pallas_call | solution.py:304
  40.8 0.0 copy-start
  40.8 3.3 %copy.11 = f32[1152,32,16]{0,2,1:T(8,128)} copy(f32[1152,32,16]{0,2,1:T(8,128)} %bitcast.6) | data formatting | bytes 4718592
  44.1 0.0 copy-done
  44.1 1.0 %copy.12 = f32[4,32,16,128]{3,2,1,0:T(8,128)} copy(f32[4,32,16,128]{3,2,1,0:T(8,128)S(1)} %copy-done) | data formatting | bytes 2097152
Async XLA Ops:
  40.8 3.3 %copy-start = (f32[4,32,16,128]{3,2,1,0:T(8,128)S(1)}, f32[4,32,16,128]{3,2,1,0:T(8,128)}, u32[]{:S(2)}) copy-start(f32[4,32,16,128]{3,2,1,0:T(8,128)} %get-tuple-element.9) | copy-start | bytes 3145732

commit v2 on v1

--- a/solution.py
+++ b/solution.py
@@ -17,6 +17,7 @@
 LANES = 128
 PITCH = 24
 LEAD = 8
+OCEAN_UNROLL = 4
 W, E, N, S = range(4)
 
 
@@ -26,7 +27,7 @@
            ebuf, xbuf, low, elow, mbuf, stok, cour, ownv, maskv, obuf,
            sea, o0, o1, ux, uy, drift,
            epack, ehx, ehy, opack, ohx, ohy,
-           lsem, esem, ersem, osem, orsem, wsem):
+           lsem, esem, ersem, osem, orsem):
     g = lax.axis_index("grp")
     t = lax.axis_index("tile")
     ng = lax.axis_size("grp")
@@ -39,6 +40,10 @@
     chunks = [(k, min(2, tiles - k)) for k in range(0, tiles, 2)]
     fields = obuf.shape[1]
 
+    def place(m, k):
+        full = tiles // 2
+        return (m * (full + 1) + k // 2, k % 2) if k < 2 * full else (full, m)
+
     e4 = ebuf.reshape(tiles, rows + 2, PITCH, LANES)
     o5 = obuf.reshape(2, fields, rows + 2, PITCH, LANES)
 
@@ -54,9 +59,12 @@
     small = [load(oc, o5.at[0, :, pl.ds(1, rows), pl.ds(LEAD, cols), :]),
              load(cour_h, cour), load(mask_h, maskv), load(own_h, ownv)]
     m_load = []
-    for k, width in chunks:
-        span = pl.ds(k * LANES, width * LANES)
-        m_load.append([load(mats.at[m, span, :], mbuf.at[span, pl.ds(m * bins, bins)]) for m in range(mats_count)])
+    for m in range(mats_count):
+        for k in range(0, tiles, 2):
+            width = min(2, tiles - k)
+            pair, half = place(m, k)
+            m_load.append(load(mats.at[m, :, pl.ds(k * LANES, width * LANES)],
+                               mbuf.at[pair, :, pl.ds(half * LANES, width * LANES)]))
     stok_load = load(stok_h, stok)
 
     barrier = pltpu.get_barrier_semaphore()
@@ -170,9 +178,14 @@
         sea[at, :] = jnp.broadcast_to(mask_all[:, r:r + 1], (cols, LANES))
         o0[at, :] = jnp.broadcast_to(own0[:, r:r + 1], (cols, LANES))
         o1[at, :] = jnp.broadcast_to(own1[:, r:r + 1], (cols, LANES))
-        for q, dst in ((0, ux), (1, uy)):
-            here = obuf[0, q, pl.ds((r + 1) * PITCH + LEAD, cols), :]
-            dst[at, :] = current_gain * jnp.broadcast_to(here[:, 0:1], (cols, LANES))
+
+    def currents(slot):
+        for r in range(rows):
+            for q, dst in ((0, ux), (1, uy)):
+                here = obuf[slot, q, pl.ds((r + 1) * PITCH + LEAD, cols), :]
+                dst[r * cols:(r + 1) * cols, :] = current_gain * jnp.broadcast_to(here[:, 0:1], (cols, LANES))
+
+    currents(0)
 
     def advect(step, k):
         cx = jnp.broadcast_to(cour[0:1, k * LANES:(k + 1) * LANES], (cols, LANES))
@@ -195,15 +208,16 @@
                 flux = flux + sy * jnp.where(sy > 0.0, mid - north, south - mid)
                 adv = sea[at, :] * (mid - flux)
                 xbuf[k, at, :] = adv
-                low[at, k * LANES:(k + 1) * LANES] = (adv * o0[at, :]).astype(jnp.bfloat16)
-                low[at, bins + k * LANES:bins + (k + 1) * LANES] = (adv * o1[at, :]).astype(jnp.bfloat16)
+                for m, chosen in ((0, o0), (1, o1)):
+                    pair, half = place(m, k)
+                    low[pair, at, half * LANES:(half + 1) * LANES] = (adv * chosen[at, :]).astype(jnp.bfloat16)
 
     lane = lax.broadcasted_iota(jnp.int32, (cols, LANES), 1)
 
     def ocean(step):
         dst_o = 1 - step
 
-        @pl.loop(0, rows)
+        @pl.loop(0, rows, unroll=OCEAN_UNROLL)
         def _(r):
             base = (r + 1) * PITCH + LEAD
             at = pl.ds(pl.multiple_of(r * cols, cols), cols)
@@ -227,12 +241,11 @@
                 else:
                     tend = mix - transport * (d0 * (0.5 * (east - west)) + d1 * (0.5 * (south - north)))
                 new = mid + sm * tend
-                obuf[dst_o, q, pl.ds(base, cols), :] = new
-                if step == 0 and q < 2:
-                    dst = (ux, uy)[q]
-                    dst[at, :] = current_gain * jnp.broadcast_to(new[:, 0:1], (cols, LANES))
-
-    out_copies = []
+                if step + 1 < STEPS:
+                    obuf[dst_o, q, pl.ds(base, cols), :] = new
+                else:
+                    o_out[q, r] = new
+
     for step in range(STEPS):
         for c, (k0, width) in enumerate(chunks):
             wait_recv(lambda d: e_arrival(step, d, c))
@@ -245,26 +258,25 @@
         for c in range(len(chunks)):
             wait_send(lambda d: e_copy(step, d, c))
         for c, (k0, width) in enumerate(chunks):
-            if step == 0:
-                for copy in m_load[c]:
+            if step == 0 and c == 0:
+                for copy in m_load:
                     copy.wait()
-            src = lax.dot_general(
-                low[...], mbuf[k0 * LANES:(k0 + width) * LANES, :], (((1,), (1,)), ((), ())),
-                preferred_element_type=jnp.float32)
+            src = 0.0
+            for pair in range(tiles):
+                src = src + lax.dot_general(
+                    low[pair], mbuf[pair, k0 * LANES:(k0 + width) * LANES, :], (((1,), (1,)), ((), ())),
+                    preferred_element_type=jnp.float32)
             for k in range(k0, k0 + width):
                 part = src[:, (k - k0) * LANES:(k - k0 + 1) * LANES]
                 new = sea[...] * (xbuf[k] + source_gain * part)
-                e4[k, 1:rows + 1, LEAD:LEAD + cols, :] = new.reshape(rows, cols, LANES)
+                if step + 1 < STEPS:
+                    e4[k, 1:rows + 1, LEAD:LEAD + cols, :] = new.reshape(rows, cols, LANES)
+                else:
+                    e_out[:, :, k * LANES:(k + 1) * LANES] = new.reshape(rows, cols, LANES)
                 elow[:, k * LANES:(k + 1) * LANES] = new.astype(jnp.bfloat16)
             if step + 1 < STEPS:
                 e_pack(step + 1, c)
                 send(lambda d: e_copy(step + 1, d, c))
-            else:
-                for k in range(k0, k0 + width):
-                    copy = pltpu.make_async_copy(
-                        e4.at[k, pl.ds(1, rows), pl.ds(LEAD, cols), :], e_out.at[:, :, pl.ds(k * LANES, LANES)], wsem.at[k])
-                    copy.start()
-                    out_copies.append(copy)
         if step == 0:
             stok_load.wait()
         drift[...] = jnp.dot(elow[...], stok[...], preferred_element_type=jnp.float32)
@@ -278,15 +290,10 @@
             wait_send(lambda d: o_copy(0, d))
         ocean(step)
         if step + 1 < STEPS:
+            currents(1 - step)
             o_pack(step + 1)
             send(lambda d: o_copy(step + 1, d))
-    copy = pltpu.make_async_copy(
-        o5.at[0, :, pl.ds(1, rows), pl.ds(LEAD, cols), :], o_out, wsem.at[tiles])
-    copy.start()
-    out_copies.append(copy)
     wait_send(lambda d: o_copy(1, d))
-    for copy in out_copies:
-        copy.wait()
 
 
 def local(spectrum, matrices, ownership, land_mask, courant, stokes_weight, ocean):
@@ -305,13 +312,13 @@
         functools.partial(kernel, rows, cols, tiles, count),
         out_shape=(jax.ShapeDtypeStruct((rows, cols, bins), f32), jax.ShapeDtypeStruct(ocean.shape, f32)),
         in_specs=[any_spec] * 7,
-        out_specs=(any_spec, any_spec),
+        out_specs=(pl.BlockSpec(memory_space=pltpu.VMEM),) * 2,
         scratch_shapes=[
             pltpu.VMEM((tiles, flat, LANES), f32),
             pltpu.VMEM((tiles, points, LANES), f32),
-            pltpu.VMEM((points, count * bins), jnp.bfloat16),
+            pltpu.VMEM((tiles, points, 2 * LANES), jnp.bfloat16),
             pltpu.VMEM((points, bins), jnp.bfloat16),
-            pltpu.VMEM((bins, count * bins), jnp.bfloat16),
+            pltpu.VMEM((tiles, bins, 2 * LANES), jnp.bfloat16),
             pltpu.VMEM((bins, 2 * LANES), jnp.bfloat16),
             pltpu.VMEM((2, bins), f32),
             pltpu.VMEM((cols, rows), jnp.int32),
@@ -330,11 +337,10 @@
             pltpu.SemaphoreType.DMA((STEPS, 4, chunk_count)),
             pltpu.SemaphoreType.DMA((STEPS, 4)),
             pltpu.SemaphoreType.DMA((STEPS, 4)),
-            pltpu.SemaphoreType.DMA((tiles + 1,)),
         ],
         compiler_params=pltpu.CompilerParams(
-            collective_id=0, has_side_effects=True, vmem_limit_bytes=56 * 1024 * 1024),
-    )(e0, mats, ownership.T, land_mask.T, courant, stokes_weight, ocean)
+            collective_id=0, has_side_effects=True, vmem_limit_bytes=34 * 1024 * 1024),
+    )(*[pltpu.with_memory_space_constraint(x, pltpu.HBM) for x in (e0, mats, ownership.T, land_mask.T, courant, stokes_weight, ocean)])
     return jnp.transpose(e_new, (2, 0, 1)), o_new
 
 

time: 45.4 us -> 35.5 us (0.78)
  Pallas kernels: 40.2 us -> 32.4 us
  local copies, waits for them, and re-layouts: 4.28 us -> 2.38 us
    pallas_call x1, Pallas kernels: 40.2 us -> 32.4 us  [local(): pl.pallas_call(functools.partial(kernel, rows, cols, tiles, count), out_s...]
    unnamed x4 -> x2, local copies, waits for them, and re-layouts: 4.28 us -> 2.38 us
where the time goes in v2:
time: 35.5 us; the launch traced here: 35.4 us
  Pallas kernels  32.4 us (91%)
  local copies, waits for them, and re-layouts  2.38 us (7%)
  between operations  0.64 us (2%)
    pallas_call x1, Pallas kernels, local(): pl.pallas_call(functools.partial(kernel, rows, cols, tiles, count), out_s...  32.4 us
    unnamed x2, local copies, waits for them, and re-layouts  2.38 us

profile of v2, /device:TPU:166, one launch (start us, length us, event | category | flops | bytes accessed | tf_op | source)
XLA Modules:
  0.0 35.4 jit_solution(10884606467175777688)
XLA Ops:
  0.6 32.4 %shard_map.86 = (f32[32,16,1152]{2,1,0:T(8,128)S(1)}, f32[4,32,16,128]{3,2,1,0:T(8,128)S(1)}) custom-call(f32[32,16,1152]{2,1,0:T(8,128)} %bitcast.7, bf16[2,1152,1152]{2,1,0:T(8,128)(2,1)} %bitcast.6, s32[16,32]{1,0:T(8,128)} %bitcast.8, s32[16,32]{1,0:T(8,128)} %bitcast.9, f32[2,1152]{1,0:T(2,128)} %cour_h.1, bf16[1152,256]{1,0:T(8,128)(2,1)} %stok_h.1, ...), custom_call_target="tpu_custom_call" | custom-call | tf_op jit(solution)/shard_map/pallas_call | solution.py:311
  33.0 1.4 %copy.11 = f32[1152,32,16]{0,2,1:T(8,128)} copy(f32[1152,32,16]{0,2,1:T(8,128)S(1)} %bitcast.5) | data formatting | bytes 4718592
  34.4 1.0 %copy.12 = f32[4,32,16,128]{3,2,1,0:T(8,128)} copy(f32[4,32,16,128]{3,2,1,0:T(8,128)S(1)} %get-tuple-element.9) | data formatting | bytes 2097152

commit v3 on v2

--- a/solution.py
+++ b/solution.py
@@ -47,6 +47,12 @@
     e4 = ebuf.reshape(tiles, rows + 2, PITCH, LANES)
     o5 = obuf.reshape(2, fields, rows + 2, PITCH, LANES)
 
+    barrier = pltpu.get_barrier_semaphore()
+    for d in range(4):
+        @pl.when(has[d])
+        def _(d=d):
+            pl.semaphore_signal(barrier, inc=1, device_id=peer[d], device_id_type=pl.DeviceIdType.MESH)
+
     loads = []
 
     def load(src, dst):
@@ -58,21 +64,6 @@
     e_load = [load(e0.at[:, :, pl.ds(k * LANES, LANES)], e4.at[k, pl.ds(1, rows), pl.ds(LEAD, cols), :]) for k in range(tiles)]
     small = [load(oc, o5.at[0, :, pl.ds(1, rows), pl.ds(LEAD, cols), :]),
              load(cour_h, cour), load(mask_h, maskv), load(own_h, ownv)]
-    m_load = []
-    for m in range(mats_count):
-        for k in range(0, tiles, 2):
-            width = min(2, tiles - k)
-            pair, half = place(m, k)
-            m_load.append(load(mats.at[m, :, pl.ds(k * LANES, width * LANES)],
-                               mbuf.at[pair, :, pl.ds(half * LANES, width * LANES)]))
-    stok_load = load(stok_h, stok)
-
-    barrier = pltpu.get_barrier_semaphore()
-    for d in range(4):
-        @pl.when(has[d])
-        def _(d=d):
-            pl.semaphore_signal(barrier, inc=1, device_id=peer[d], device_id_type=pl.DeviceIdType.MESH)
-
     for d in range(4):
         @pl.when(jnp.logical_not(has[d]))
         def _(d=d):
@@ -140,7 +131,7 @@
             opack[step, E, q] = obuf[step, q, last_col, :]
 
     def send(make):
-        for d in range(4):
+        for d in (N, S, W, E):
             @pl.when(has[d])
             def _(d=d):
                 make(d).start()
@@ -161,8 +152,16 @@
         for k in range(k0, k0 + width):
             e_load[k].wait()
         e_pack(0, c)
-        if c == 0:
-            pl.semaphore_wait(barrier, sum(h.astype(jnp.int32) for h in has))
+    m_load = []
+    for m in range(mats_count):
+        for k in range(0, tiles, 2):
+            width = min(2, tiles - k)
+            pair, half = place(m, k)
+            m_load.append(load(mats.at[m, :, pl.ds(k * LANES, width * LANES)],
+                               mbuf.at[pair, :, pl.ds(half * LANES, width * LANES)]))
+    stok_load = load(stok_h, stok)
+    pl.semaphore_wait(barrier, sum(h.astype(jnp.int32) for h in has))
+    for c in range(len(chunks)):
         send(lambda d: e_copy(0, d, c))
     for copy in small:
         copy.wait()
@@ -187,27 +186,40 @@
 
     currents(0)
 
-    def advect(step, k):
-        cx = jnp.broadcast_to(cour[0:1, k * LANES:(k + 1) * LANES], (cols, LANES))
-        cy = jnp.broadcast_to(cour[1:2, k * LANES:(k + 1) * LANES], (cols, LANES))
-
+    def advect(k, base, at, stride=None):
+        count = cols if stride is None else rows
+
+        def near(shift):
+            return ebuf[k, pl.ds(base + shift, count, stride=None if stride is None else PITCH), :]
+
+        cx = jnp.broadcast_to(cour[0:1, k * LANES:(k + 1) * LANES], (count, LANES))
+        cy = jnp.broadcast_to(cour[1:2, k * LANES:(k + 1) * LANES], (count, LANES))
+        mid = near(0)
+        sx = cx + ux[at, :]
+        sy = cy + uy[at, :]
+        flux = sx * jnp.where(sx > 0.0, mid - near(-1), near(1) - mid)
+        flux = flux + sy * jnp.where(sy > 0.0, mid - near(-PITCH), near(PITCH) - mid)
+        xbuf[k, at, :] = sea[at, :] * (mid - flux)
+
+    def advect_all(k):
         @pl.loop(0, rows // 8)
         def _(block):
             for i in range(8):
                 r = block * 8 + i
-                base = (r + 1) * PITCH + LEAD
-                at = pl.ds(pl.multiple_of(r * cols, cols), cols)
-                mid = ebuf[k, pl.ds(base, cols), :]
-                west = ebuf[k, pl.ds(base - 1, cols), :]
-                east = ebuf[k, pl.ds(base + 1, cols), :]
-                north = ebuf[k, pl.ds(base - PITCH, cols), :]
-                south = ebuf[k, pl.ds(base + PITCH, cols), :]
-                sx = cx + ux[at, :]
-                sy = cy + uy[at, :]
-                flux = sx * jnp.where(sx > 0.0, mid - west, east - mid)
-                flux = flux + sy * jnp.where(sy > 0.0, mid - north, south - mid)
-                adv = sea[at, :] * (mid - flux)
-                xbuf[k, at, :] = adv
+                advect(k, (r + 1) * PITCH + LEAD, pl.ds(pl.multiple_of(r * cols, cols), cols))
+
+    def advect_border(k):
+        for r in (0, rows - 1):
+            advect(k, (r + 1) * PITCH + LEAD, pl.ds(r * cols, cols))
+        for c in (0, cols - 1):
+            advect(k, PITCH + LEAD + c, pl.ds(c, rows, stride=cols), cols)
+
+    def lower(k):
+        @pl.loop(0, rows // 8)
+        def _(block):
+            for i in range(8):
+                at = pl.ds(pl.multiple_of((block * 8 + i) * cols, cols), cols)
+                adv = xbuf[k, at, :]
                 for m, chosen in ((0, o0), (1, o1)):
                     pair, half = place(m, k)
                     low[pair, at, half * LANES:(half + 1) * LANES] = (adv * chosen[at, :]).astype(jnp.bfloat16)
@@ -247,6 +259,8 @@
                     o_out[q, r] = new
 
     for step in range(STEPS):
+        for k in range(tiles):
+            advect_all(k)
         for c, (k0, width) in enumerate(chunks):
             wait_recv(lambda d: e_arrival(step, d, c))
             for k in range(k0, k0 + width):
@@ -254,7 +268,8 @@
                 ebuf[k, east_col, :] = ehx[step, E, k]
                 ebuf[k, pl.ds(LEAD, cols), :] = ehy[step, 0, k]
                 ebuf[k, pl.ds((rows + 1) * PITCH + LEAD, cols), :] = ehy[step, 1, k]
-                advect(step, k)
+                advect_border(k)
+                lower(k)
         for c in range(len(chunks)):
             wait_send(lambda d: e_copy(step, d, c))
         for c, (k0, width) in enumerate(chunks):

time: 35.5 us -> 34.3 us (0.966)
  Pallas kernels: 32.4 us -> 31.2 us
    pallas_call x1, Pallas kernels: 32.4 us -> 31.2 us  [local(): pl.pallas_call(functools.partial(kernel, rows, cols, tiles, count), out_s...]
where the time goes in v3:
time: 34.3 us; the launch traced here: 34.2 us
  Pallas kernels  31.2 us (91%)
  local copies, waits for them, and re-layouts  2.38 us (7%)
  between operations  0.64 us (2%)
    pallas_call x1, Pallas kernels, local(): pl.pallas_call(functools.partial(kernel, rows, cols, tiles, count), out_s...  31.2 us
    unnamed x2, local copies, waits for them, and re-layouts  2.38 us

profile of v3, /device:TPU:166, one launch (start us, length us, event | category | flops | bytes accessed | tf_op | source)
XLA Modules:
  0.0 34.2 jit_solution(4544097092228171674)
XLA Ops:
  0.6 31.2 %shard_map.86 = (f32[32,16,1152]{2,1,0:T(8,128)S(1)}, f32[4,32,16,128]{3,2,1,0:T(8,128)S(1)}) custom-call(f32[32,16,1152]{2,1,0:T(8,128)} %bitcast.7, bf16[2,1152,1152]{2,1,0:T(8,128)(2,1)} %bitcast.6, s32[16,32]{1,0:T(8,128)} %bitcast.8, s32[16,32]{1,0:T(8,128)} %bitcast.9, f32[2,1152]{1,0:T(2,128)} %cour_h.1, bf16[1152,256]{1,0:T(8,128)(2,1)} %stok_h.1, ...), custom_call_target="tpu_custom_call" | custom-call | tf_op jit(solution)/shard_map/pallas_call | solution.py:326
  31.8 1.4 %copy.11 = f32[1152,32,16]{0,2,1:T(8,128)} copy(f32[1152,32,16]{0,2,1:T(8,128)S(1)} %bitcast.5) | data formatting | bytes 4718592
  33.2 1.0 %copy.12 = f32[4,32,16,128]{3,2,1,0:T(8,128)} copy(f32[4,32,16,128]{3,2,1,0:T(8,128)S(1)} %get-tuple-element.9) | data formatting | bytes 2097152

commit v4 on v3

--- a/solution.py
+++ b/solution.py
@@ -21,11 +21,65 @@
 W, E, N, S = range(4)
 
 
+def ocean_rows(obuf, drift, sea, first, last, cols, put):
+    fields = obuf.shape[0]
+    lane = lax.broadcasted_iota(jnp.int32, (cols, LANES), 1)
+
+    @pl.loop(first, last, unroll=OCEAN_UNROLL)
+    def _(r):
+        base = (r + 1) * PITCH + LEAD
+        at = pl.ds(pl.multiple_of(r * cols, cols), cols)
+        d0 = drift[at, 0:LANES]
+        d1 = drift[at, LANES:2 * LANES]
+        sm = sea[at, :]
+        mids = [obuf[q, pl.ds(base, cols), :] for q in range(fields)]
+        for q in range(fields):
+            mid = mids[q]
+            west = obuf[q, pl.ds(base - 1, cols), :]
+            east = obuf[q, pl.ds(base + 1, cols), :]
+            north = obuf[q, pl.ds(base - PITCH, cols), :]
+            south = obuf[q, pl.ds(base + PITCH, cols), :]
+            above = jnp.where(lane == LANES - 1, 0.0, pltpu.roll(mid, LANES - 1, 1))
+            below = jnp.where(lane == 0, 0.0, pltpu.roll(mid, 1, 1))
+            mix = mixing_side * (north + south + west + east - 4.0 * mid) + mixing_depth * (above + below - 2.0 * mid)
+            if q == 0:
+                tend = mix + rotation * (mids[1] + d1)
+            elif q == 1:
+                tend = mix - rotation * (mids[0] + d0)
+            else:
+                tend = mix - transport * (d0 * (0.5 * (east - west)) + d1 * (0.5 * (south - north)))
+            put(q, r, at, base, mid + sm * tend)
+
+
+def last_kernel(rows, cols, e_new, obuf, drift, sea, e_out, o_out, stage, sem):
+    copies = []
+    blocks = 4
+    size = rows // blocks
+
+    def out(src, dst):
+        copy = pltpu.make_async_copy(src, dst, sem.at[len(copies)])
+        copy.start()
+        copies.append(copy)
+
+    def put(q, r, at, base, new):
+        stage[q, r] = new
+
+    for i in range(blocks):
+        span = pl.ds(i * size, size)
+        out(e_new.at[span], e_out.at[span])
+    for i in range(blocks):
+        span = pl.ds(i * size, size)
+        ocean_rows(obuf, drift, sea, i * size, (i + 1) * size, cols, put)
+        out(stage.at[:, span], o_out.at[:, span])
+    for copy in copies:
+        copy.wait()
+
+
 def kernel(rows, cols, tiles, mats_count,
            e0, mats, own_h, mask_h, cour_h, stok_h, oc,
-           e_out, o_out,
-           ebuf, xbuf, low, elow, mbuf, stok, cour, ownv, maskv, obuf,
-           sea, o0, o1, ux, uy, drift,
+           e_out, obuf1, drift, sea,
+           ebuf, xbuf, low, elow, mbuf, stok, cour, ownv, maskv, obuf0,
+           o0, o1, ux, uy,
            epack, ehx, ehy, opack, ohx, ohy,
            lsem, esem, ersem, osem, orsem):
     g = lax.axis_index("grp")
@@ -38,14 +92,15 @@
     peer = [{"grp": g - 1}, {"grp": g + 1}, {"tile": t - 1}, {"tile": t + 1}]
     back = [E, W, S, N]
     chunks = [(k, min(2, tiles - k)) for k in range(0, tiles, 2)]
-    fields = obuf.shape[1]
+    obuf = (obuf0, obuf1)
+    fields = obuf0.shape[0]
 
     def place(m, k):
         full = tiles // 2
         return (m * (full + 1) + k // 2, k % 2) if k < 2 * full else (full, m)
 
     e4 = ebuf.reshape(tiles, rows + 2, PITCH, LANES)
-    o5 = obuf.reshape(2, fields, rows + 2, PITCH, LANES)
+    o4 = [o.reshape(fields, rows + 2, PITCH, LANES) for o in obuf]
 
     barrier = pltpu.get_barrier_semaphore()
     for d in range(4):
@@ -62,7 +117,7 @@
         return copy
 
     e_load = [load(e0.at[:, :, pl.ds(k * LANES, LANES)], e4.at[k, pl.ds(1, rows), pl.ds(LEAD, cols), :]) for k in range(tiles)]
-    small = [load(oc, o5.at[0, :, pl.ds(1, rows), pl.ds(LEAD, cols), :]),
+    small = [load(oc, o4[0].at[:, pl.ds(1, rows), pl.ds(LEAD, cols), :]),
              load(cour_h, cour), load(mask_h, maskv), load(own_h, ownv)]
     for d in range(4):
         @pl.when(jnp.logical_not(has[d]))
@@ -102,7 +157,7 @@
             src = opack.at[step, d]
             dst = ohx.at[step, far]
         else:
-            src = o5.at[step, :, 1 if d == N else rows, pl.ds(LEAD, cols), :]
+            src = o4[step].at[:, 1 if d == N else rows, pl.ds(LEAD, cols), :]
             dst = ohy.at[step, far - 2]
         return pltpu.make_async_remote_copy(
             src_ref=src, dst_ref=dst, send_sem=osem.at[step, d], recv_sem=orsem.at[step, far],
@@ -127,8 +182,8 @@
 
     def o_pack(step):
         for q in range(fields):
-            opack[step, W, q] = obuf[step, q, first_col, :]
-            opack[step, E, q] = obuf[step, q, last_col, :]
+            opack[step, W, q] = obuf[step][q, first_col, :]
+            opack[step, E, q] = obuf[step][q, last_col, :]
 
     def send(make):
         for d in (N, S, W, E):
@@ -181,7 +236,7 @@
     def currents(slot):
         for r in range(rows):
             for q, dst in ((0, ux), (1, uy)):
-                here = obuf[slot, q, pl.ds((r + 1) * PITCH + LEAD, cols), :]
+                here = obuf[slot][q, pl.ds((r + 1) * PITCH + LEAD, cols), :]
                 dst[r * cols:(r + 1) * cols, :] = current_gain * jnp.broadcast_to(here[:, 0:1], (cols, LANES))
 
     currents(0)
@@ -224,39 +279,8 @@
                     pair, half = place(m, k)
                     low[pair, at, half * LANES:(half + 1) * LANES] = (adv * chosen[at, :]).astype(jnp.bfloat16)
 
-    lane = lax.broadcasted_iota(jnp.int32, (cols, LANES), 1)
-
-    def ocean(step):
-        dst_o = 1 - step
-
-        @pl.loop(0, rows, unroll=OCEAN_UNROLL)
-        def _(r):
-            base = (r + 1) * PITCH + LEAD
-            at = pl.ds(pl.multiple_of(r * cols, cols), cols)
-            d0 = drift[at, 0:LANES]
-            d1 = drift[at, LANES:2 * LANES]
-            sm = sea[at, :]
-            mids = [obuf[step, q, pl.ds(base, cols), :] for q in range(fields)]
-            for q in range(fields):
-                mid = mids[q]
-                west = obuf[step, q, pl.ds(base - 1, cols), :]
-                east = obuf[step, q, pl.ds(base + 1, cols), :]
-                north = obuf[step, q, pl.ds(base - PITCH, cols), :]
-                south = obuf[step, q, pl.ds(base + PITCH, cols), :]
-                above = jnp.where(lane == LANES - 1, 0.0, pltpu.roll(mid, LANES - 1, 1))
-                below = jnp.where(lane == 0, 0.0, pltpu.roll(mid, 1, 1))
-                mix = mixing_side * (north + south + west + east - 4.0 * mid) + mixing_depth * (above + below - 2.0 * mid)
-                if q == 0:
-                    tend = mix + rotation * (mids[1] + d1)
-                elif q == 1:
-                    tend = mix - rotation * (mids[0] + d0)
-                else:
-                    tend = mix - transport * (d0 * (0.5 * (east - west)) + d1 * (0.5 * (south - north)))
-                new = mid + sm * tend
-                if step + 1 < STEPS:
-                    obuf[dst_o, q, pl.ds(base, cols), :] = new
-                else:
-                    o_out[q, r] = new
+    def put(q, base, new):
+        obuf[1][q, pl.ds(base, cols), :] = new
 
     for step in range(STEPS):
         for k in range(tiles):
@@ -297,14 +321,14 @@
         drift[...] = jnp.dot(elow[...], stok[...], preferred_element_type=jnp.float32)
         wait_recv(lambda d: o_arrival(step, d))
         for q in range(fields):
-            obuf[step, q, west_col, :] = ohx[step, W, q]
-            obuf[step, q, east_col, :] = ohx[step, E, q]
-            obuf[step, q, pl.ds(LEAD, cols), :] = ohy[step, 0, q]
-            obuf[step, q, pl.ds((rows + 1) * PITCH + LEAD, cols), :] = ohy[step, 1, q]
+            obuf[step][q, west_col, :] = ohx[step, W, q]
+            obuf[step][q, east_col, :] = ohx[step, E, q]
+            obuf[step][q, pl.ds(LEAD, cols), :] = ohy[step, 0, q]
+            obuf[step][q, pl.ds((rows + 1) * PITCH + LEAD, cols), :] = ohy[step, 1, q]
         if step == 1:
             wait_send(lambda d: o_copy(0, d))
-        ocean(step)
         if step + 1 < STEPS:
+            ocean_rows(obuf[0], drift, sea, 0, rows, cols, lambda q, r, at, base, new: put(q, base, new))
             currents(1 - step)
             o_pack(step + 1)
             send(lambda d: o_copy(step + 1, d))
@@ -323,11 +347,12 @@
     e0 = jnp.transpose(spectrum, (1, 2, 0))
     f32 = jnp.float32
     any_spec = pl.BlockSpec(memory_space=pltpu.HBM)
-    e_new, o_new = pl.pallas_call(
+    e_new, o_mid, drift, sea = pl.pallas_call(
         functools.partial(kernel, rows, cols, tiles, count),
-        out_shape=(jax.ShapeDtypeStruct((rows, cols, bins), f32), jax.ShapeDtypeStruct(ocean.shape, f32)),
+        out_shape=(jax.ShapeDtypeStruct((rows, cols, bins), f32), jax.ShapeDtypeStruct((fields, flat, LANES), f32),
+                   jax.ShapeDtypeStruct((points, 2 * LANES), f32), jax.ShapeDtypeStruct((points, LANES), f32)),
         in_specs=[any_spec] * 7,
-        out_specs=(pl.BlockSpec(memory_space=pltpu.VMEM),) * 2,
+        out_specs=(pl.BlockSpec(memory_space=pltpu.VMEM),) * 4,
         scratch_shapes=[
             pltpu.VMEM((tiles, flat, LANES), f32),
             pltpu.VMEM((tiles, points, LANES), f32),
@@ -338,9 +363,8 @@
             pltpu.VMEM((2, bins), f32),
             pltpu.VMEM((cols, rows), jnp.int32),
             pltpu.VMEM((cols, rows), jnp.int32),
-            pltpu.VMEM((2, fields, flat, LANES), f32),
-        ] + [pltpu.VMEM((points, LANES), f32)] * 5 + [
-            pltpu.VMEM((points, 2 * LANES), f32),
+            pltpu.VMEM((fields, flat, LANES), f32),
+        ] + [pltpu.VMEM((points, LANES), f32)] * 4 + [
             pltpu.VMEM((STEPS, 2, tiles, rows, LANES), f32),
             pltpu.VMEM((STEPS, 2, tiles, rows, LANES), f32),
             pltpu.VMEM((STEPS, 2, tiles, cols, LANES), f32),
@@ -356,7 +380,15 @@
         compiler_params=pltpu.CompilerParams(
             collective_id=0, has_side_effects=True, vmem_limit_bytes=34 * 1024 * 1024),
     )(*[pltpu.with_memory_space_constraint(x, pltpu.HBM) for x in (e0, mats, ownership.T, land_mask.T, courant, stokes_weight, ocean)])
-    return jnp.transpose(e_new, (2, 0, 1)), o_new
+    e_out, o_new = pl.pallas_call(
+        functools.partial(last_kernel, rows, cols),
+        out_shape=(jax.ShapeDtypeStruct((rows, cols, bins), f32), jax.ShapeDtypeStruct(ocean.shape, f32)),
+        in_specs=[pl.BlockSpec(memory_space=pltpu.VMEM)] * 4,
+        out_specs=(any_spec, any_spec),
+        scratch_shapes=[pltpu.VMEM(ocean.shape, f32), pltpu.SemaphoreType.DMA((8,))],
+        compiler_params=pltpu.CompilerParams(vmem_limit_bytes=16 * 1024 * 1024),
+    )(e_new, o_mid, drift, sea)
+    return jnp.transpose(e_out, (2, 0, 1)), o_new
 
 
 def solution(mesh):

time: 34.3 us -> 32.7 us (0.953)
  local copies, waits for them, and re-layouts: 2.38 us -> 0 us
  Pallas kernels: 31.2 us -> 32 us
    unnamed x2 -> x0, local copies, waits for them, and re-layouts: 2.38 us -> none
    pallas_call x0 -> x1, Pallas kernels: none -> 1.96 us  [local(): pl.pallas_call(functools.partial(last_kernel, rows, cols), out_shape=(jax...]
    pallas_call x1, Pallas kernels: 31.2 us -> 30 us  [local(): pl.pallas_call(functools.partial(kernel, rows, cols, tiles, count), out_s...]
where the time goes in v4:
time: 32.7 us; the launch traced here: 32.6 us
  Pallas kernels  32 us (98%)
  between operations  0.64 us (2%)
    pallas_call x1, Pallas kernels, local(): pl.pallas_call(functools.partial(kernel, rows, cols, tiles, count), out_s...  30 us
    pallas_call x1, Pallas kernels, local(): pl.pallas_call(functools.partial(last_kernel, rows, cols), out_shape=(jax...  1.96 us

profile of v4, /device:TPU:166, one launch (start us, length us, event | category | flops | bytes accessed | tf_op | source)
XLA Modules:
  0.0 32.6 jit_solution(13756149243443590166)
XLA Ops:
  0.6 30.0 %shard_map.86 = (f32[32,16,1152]{2,1,0:T(8,128)S(1)}, f32[4,816,128]{2,1,0:T(8,128)S(1)}, f32[512,256]{1,0:T(8,128)S(1)}, f32[512,128]{1,0:T(8,128)S(1)}) custom-call(f32[32,16,1152]{2,1,0:T(8,128)} %bitcast.6, bf16[2,1152,1152]{2,1,0:T(8,128)(2,1)} %bitcast.5, s32[16,32]{1,0:T(8,128)} %bitcast.7, s32[16,32]{1,0:T(8,128)} %bitcast.8, f32[2,1152]{1,0:T(2,128)} %cour_h.1, ...), custom_call_target="tpu_custom_call" | custom-call | tf_op jit(solution)/shard_map/pallas_call | solution.py:350
  30.7 2.0 %shard_map.87 = (f32[32,16,1152]{2,1,0:T(8,128)}, f32[4,32,16,128]{3,2,1,0:T(8,128)}) custom-call(f32[32,16,1152]{2,1,0:T(8,128)S(1)} %get-tuple-element.8.e_new, f32[4,816,128]{2,1,0:T(8,128)S(1)} %get-tuple-element.9.obuf, f32[512,256]{1,0:T(8,128)S(1)} %get-tuple-element.10.drift, f32[512,128]{1,0:T(8,128)S(1)} %get-tuple-element.11.sea), custom_call_target="tpu_custom_call" | custom-call | tf_op jit(solution)/shard_map/pallas_call | solution.py:383

commit v5 on v4

--- a/solution.py
+++ b/solution.py
@@ -79,7 +79,7 @@
            e0, mats, own_h, mask_h, cour_h, stok_h, oc,
            e_out, obuf1, drift, sea,
            ebuf, xbuf, low, elow, mbuf, stok, cour, ownv, maskv, obuf0,
-           o0, o1, ux, uy,
+           o0, o1, ux, uy, acc,
            epack, ehx, ehy, opack, ohx, ohy,
            lsem, esem, ersem, osem, orsem):
     g = lax.axis_index("grp")
@@ -279,6 +279,25 @@
                     pair, half = place(m, k)
                     low[pair, at, half * LANES:(half + 1) * LANES] = (adv * chosen[at, :]).astype(jnp.bfloat16)
 
+    def gather(c, first_tile):
+        pairs = sorted({place(m, first_tile)[0] for m in range(mats_count)})
+        for k0, width in chunks:
+            src = 0.0
+            for pair in pairs:
+                src = src + lax.dot_general(
+                    low[pair], mbuf[pair, k0 * LANES:(k0 + width) * LANES, :], (((1,), (1,)), ((), ())),
+                    preferred_element_type=jnp.float32)
+            for k in range(k0, k0 + width):
+                part = src[:, (k - k0) * LANES:(k - k0 + 1) * LANES]
+                if c > 0:
+                    part = part + acc[k]
+                if c + 1 < len(chunks):
+                    acc[k] = part
+                else:
+                    new = sea[...] * (xbuf[k] + source_gain * part)
+                    e_out[:, :, k * LANES:(k + 1) * LANES] = new.reshape(rows, cols, LANES)
+                    elow[:, k * LANES:(k + 1) * LANES] = new.astype(jnp.bfloat16)
+
     def put(q, base, new):
         obuf[1][q, pl.ds(base, cols), :] = new
 
@@ -294,9 +313,11 @@
                 ebuf[k, pl.ds((rows + 1) * PITCH + LEAD, cols), :] = ehy[step, 1, k]
                 advect_border(k)
                 lower(k)
+            if step + 1 == STEPS:
+                gather(c, k0)
         for c in range(len(chunks)):
             wait_send(lambda d: e_copy(step, d, c))
-        for c, (k0, width) in enumerate(chunks):
+        for c, (k0, width) in enumerate(chunks if step + 1 < STEPS else []):
             if step == 0 and c == 0:
                 for copy in m_load:
                     copy.wait()
@@ -308,10 +329,7 @@
             for k in range(k0, k0 + width):
                 part = src[:, (k - k0) * LANES:(k - k0 + 1) * LANES]
                 new = sea[...] * (xbuf[k] + source_gain * part)
-                if step + 1 < STEPS:
-                    e4[k, 1:rows + 1, LEAD:LEAD + cols, :] = new.reshape(rows, cols, LANES)
-                else:
-                    e_out[:, :, k * LANES:(k + 1) * LANES] = new.reshape(rows, cols, LANES)
+                e4[k, 1:rows + 1, LEAD:LEAD + cols, :] = new.reshape(rows, cols, LANES)
                 elow[:, k * LANES:(k + 1) * LANES] = new.astype(jnp.bfloat16)
             if step + 1 < STEPS:
                 e_pack(step + 1, c)
@@ -365,6 +383,7 @@
             pltpu.VMEM((cols, rows), jnp.int32),
             pltpu.VMEM((fields, flat, LANES), f32),
         ] + [pltpu.VMEM((points, LANES), f32)] * 4 + [
+            pltpu.VMEM((tiles, points, LANES), f32),
             pltpu.VMEM((STEPS, 2, tiles, rows, LANES), f32),
             pltpu.VMEM((STEPS, 2, tiles, rows, LANES), f32),
             pltpu.VMEM((STEPS, 2, tiles, cols, LANES), f32),

time: 32.7 us -> 33.7 us (1.031)
  Pallas kernels: 32 us -> 32.9 us
    pallas_call x1, Pallas kernels: 30 us -> 31 us  [local(): pl.pallas_call(functools.partial(kernel, rows, cols, tiles, count), out_s...]
where the time goes in v5:
time: 33.7 us; the launch traced here: 33.6 us
  Pallas kernels  32.9 us (98%)
  between operations  0.64 us (2%)
    pallas_call x1, Pallas kernels, local(): pl.pallas_call(functools.partial(kernel, rows, cols, tiles, count), out_s...  31 us
    pallas_call x1, Pallas kernels, local(): pl.pallas_call(functools.partial(last_kernel, rows, cols), out_shape=(jax...  1.96 us

profile of v5, /device:TPU:166, one launch (start us, length us, event | category | flops | bytes accessed | tf_op | source)
XLA Modules:
  0.0 33.6 jit_solution(11515365103392670268)
XLA Ops:
  0.6 31.0 %shard_map.86 = (f32[32,16,1152]{2,1,0:T(8,128)S(1)}, f32[4,816,128]{2,1,0:T(8,128)S(1)}, f32[512,256]{1,0:T(8,128)S(1)}, f32[512,128]{1,0:T(8,128)S(1)}) custom-call(f32[32,16,1152]{2,1,0:T(8,128)} %bitcast.6, bf16[2,1152,1152]{2,1,0:T(8,128)(2,1)} %bitcast.5, s32[16,32]{1,0:T(8,128)} %bitcast.7, s32[16,32]{1,0:T(8,128)} %bitcast.8, f32[2,1152]{1,0:T(2,128)} %cour_h.1, ...), custom_call_target="tpu_custom_call" | custom-call | tf_op jit(solution)/shard_map/pallas_call | solution.py:368
  31.6 2.0 %shard_map.87 = (f32[32,16,1152]{2,1,0:T(8,128)}, f32[4,32,16,128]{3,2,1,0:T(8,128)}) custom-call(f32[32,16,1152]{2,1,0:T(8,128)S(1)} %get-tuple-element.8.e_new, f32[4,816,128]{2,1,0:T(8,128)S(1)} %get-tuple-element.9.obuf, f32[512,256]{1,0:T(8,128)S(1)} %get-tuple-element.10.drift, f32[512,128]{1,0:T(8,128)S(1)} %get-tuple-element.11.sea), custom_call_target="tpu_custom_call" | custom-call | tf_op jit(solution)/shard_map/pallas_call | solution.py:402

commit v6 on v4

--- a/solution.py
+++ b/solution.py
@@ -130,7 +130,7 @@
                 ohy[:, d - 2] = jnp.zeros_like(ohy[:, d - 2])
 
     def e_copy(step, d, c):
-        k, width = chunks[c]
+        k, width = chunks[c] if step else (0, tiles)
         span = pl.ds(k, width)
         far = back[d]
         if d < 2:
@@ -144,7 +144,7 @@
             device_id=peer[d], device_id_type=pl.DeviceIdType.MESH)
 
     def e_arrival(step, side, c):
-        k, width = chunks[c]
+        k, width = chunks[c] if step else (0, tiles)
         span = pl.ds(k, width)
         dst = ehx.at[step, side, span] if side < 2 else ehy.at[step, side - 2, span]
         return pltpu.make_async_remote_copy(
@@ -216,8 +216,7 @@
                                mbuf.at[pair, :, pl.ds(half * LANES, width * LANES)]))
     stok_load = load(stok_h, stok)
     pl.semaphore_wait(barrier, sum(h.astype(jnp.int32) for h in has))
-    for c in range(len(chunks)):
-        send(lambda d: e_copy(0, d, c))
+    send(lambda d: e_copy(0, d, 0))
     for copy in small:
         copy.wait()
     o_pack(0)
@@ -286,7 +285,8 @@
         for k in range(tiles):
             advect_all(k)
         for c, (k0, width) in enumerate(chunks):
-            wait_recv(lambda d: e_arrival(step, d, c))
+            if step or c == 0:
+                wait_recv(lambda d: e_arrival(step, d, c))
             for k in range(k0, k0 + width):
                 ebuf[k, west_col, :] = ehx[step, W, k]
                 ebuf[k, east_col, :] = ehx[step, E, k]
@@ -294,7 +294,7 @@
                 ebuf[k, pl.ds((rows + 1) * PITCH + LEAD, cols), :] = ehy[step, 1, k]
                 advect_border(k)
                 lower(k)
-        for c in range(len(chunks)):
+        for c in range(len(chunks) if step else 1):
             wait_send(lambda d: e_copy(step, d, c))
         for c, (k0, width) in enumerate(chunks):
             if step == 0 and c == 0:

time: 32.7 us -> 33.5 us (1.024)
  the two profiles are of different devices: /device:TPU:166 before, /device:TPU:197 now
where the time goes in v6:
time: 33.5 us; the launch traced here: 33.4 us
  Pallas kernels  32.8 us (98%)
  between operations  0.64 us (2%)
    pallas_call x1, Pallas kernels, local(): pl.pallas_call(functools.partial(kernel, rows, cols, tiles, count), out_s...  30.8 us
    pallas_call x1, Pallas kernels, local(): pl.pallas_call(functools.partial(last_kernel, rows, cols), out_shape=(jax...  1.96 us

profile of v6, /device:TPU:197, one launch (start us, length us, event | category | flops | bytes accessed | tf_op | source)
XLA Modules:
  0.0 33.4 jit_solution(14866187530522130282)
XLA Ops:
  0.6 30.8 %shard_map.86 = (f32[32,16,1152]{2,1,0:T(8,128)S(1)}, f32[4,816,128]{2,1,0:T(8,128)S(1)}, f32[512,256]{1,0:T(8,128)S(1)}, f32[512,128]{1,0:T(8,128)S(1)}) custom-call(f32[32,16,1152]{2,1,0:T(8,128)} %bitcast.6, bf16[2,1152,1152]{2,1,0:T(8,128)(2,1)} %bitcast.5, s32[16,32]{1,0:T(8,128)} %bitcast.7, s32[16,32]{1,0:T(8,128)} %bitcast.8, f32[2,1152]{1,0:T(2,128)} %cour_h.1, ...), custom_call_target="tpu_custom_call" | custom-call | tf_op jit(solution)/shard_map/pallas_call | solution.py:350
  31.5 2.0 %shard_map.87 = (f32[32,16,1152]{2,1,0:T(8,128)}, f32[4,32,16,128]{3,2,1,0:T(8,128)}) custom-call(f32[32,16,1152]{2,1,0:T(8,128)S(1)} %get-tuple-element.8.e_new, f32[4,816,128]{2,1,0:T(8,128)S(1)} %get-tuple-element.9.obuf, f32[512,256]{1,0:T(8,128)S(1)} %get-tuple-element.10.drift, f32[512,128]{1,0:T(8,128)S(1)} %get-tuple-element.11.sea), custom_call_target="tpu_custom_call" | custom-call | tf_op jit(solution)/shard_map/pallas_call | solution.py:383
